TPU v7x, 32 devices: a whole 2x2x4 slice. The times are simulated.
32 devices in a mesh: job: 2 (over x), tm: 2 (over core), rows: 8 (over z, y).
Axes of the slice: x: 2, y: 2, z: 4, core: 2. Of those that a mesh axis runs over, the one named last changes fastest.
Arguments:
- prior: bfloat16 [2, 524288, 64], P('tm', ('job', 'rows')), parts along dimension 1, may hold values from -80 to 80
- snapshots: bfloat16 [2, 524288, 256], P('tm', ('job', 'rows')), parts along dimension 1, may hold values from -60 to 60
Outputs:
- merged: bfloat16 [524288, 64], P(('job', 'rows'), 'tm'), parts along dimension 0
There are 2 independent parts, one for each index of `job`. A program takes and returns all parts, laid end to end along the dimension named above; each array names one. Nothing has to cross between parts.
All inputs are finite; a program needn't handle non-finite values.
Results may differ from a plain program's by a relative error of at most 0.011.
Values may be sent and summed in bfloat16 or wider, within the bound.
No kernel may reach another device: no remote copies, remote signals or barrier semaphores. Data moves between devices by JAX's collectives and lax.ppermute only.
A program may use at most 128 MiB of HBM per device.

v0:
```python
import jax
import jax.numpy as jnp
from jax import lax
from jax.sharding import PartitionSpec as P

STEPS = 4
ITERS = 2


def partner(block, axis, bit):
    count = lax.axis_size(axis)
    route = []
    for low in range(count):
        high = low | 1 << bit
        if high != low and high < count:
            route += [(low, high), (high, low)]
    return lax.ppermute(block, axis, route)


def basis_of(gram, keep):
    order = gram.shape[0]
    basis = jnp.eye(order, keep, dtype=jnp.float32)
    for turn in range(ITERS):
        image = jnp.dot(gram, basis, precision=lax.Precision.HIGHEST)
        inner = jnp.dot(image.T, image, precision=lax.Precision.HIGHEST)
        lower = jnp.linalg.cholesky(inner)
        basis = jax.scipy.linalg.solve_triangular(lower, image.T, lower=True).T
    return basis


def project(joined, basis):
    return jnp.dot(
        joined, basis, precision=lax.Precision.HIGHEST, preferred_element_type=jnp.float32
    )


def inner_rows(left, right):
    return jnp.dot(
        left.T, right, precision=lax.Precision.HIGHEST, preferred_element_type=jnp.float32
    )


def shards(prior, snapshots):
    start_modes = prior[0]
    frames = snapshots[0]
    keep = start_modes.shape[1]
    fresh_cols = frames.shape[1] // STEPS
    whole = jnp.concatenate([start_modes, frames], axis=1)
    total = lax.psum(jnp.dot(whole.T, whole, preferred_element_type=jnp.float32), "rows")
    width = whole.shape[1]
    weights = jnp.eye(width, keep, dtype=jnp.float32)
    for step in range(STEPS):
        picker = jnp.eye(width, fresh_cols, k=-(keep + step * fresh_cols), dtype=jnp.float32)
        coeffs = jnp.concatenate([weights, picker], axis=1)
        applied = jnp.dot(total, coeffs, precision=lax.Precision.HIGHEST)
        gram = jnp.dot(coeffs.T, applied, precision=lax.Precision.HIGHEST)
        weights = jnp.dot(coeffs, basis_of(gram, keep), precision=lax.Precision.HIGHEST)
    modes = project(whole, weights)
    index = lax.axis_index("tm")
    half_keep = keep // 2
    other = partner(modes.astype(jnp.bfloat16), "tm", 0).astype(modes.dtype)
    first = jnp.where(index == 0, modes, other)
    second = jnp.where(index == 0, other, modes)
    joined = jnp.concatenate([first, second], axis=1)
    gram = lax.psum(inner_rows(joined, joined).astype(jnp.bfloat16), "rows").astype(jnp.float32)
    full_merge = project(joined, basis_of(gram, keep)).astype(jnp.bfloat16)
    merged = lax.dynamic_slice_in_dim(full_merge, index * half_keep, half_keep, 1)
    return merged


def solution(mesh):
    in_specs = (P("tm", ("job", "rows"), None), P("tm", ("job", "rows"), None))
    out_specs = P(("job", "rows"), "tm")
    return jax.shard_map(shards, mesh=mesh, in_specs=in_specs, out_specs=out_specs, check_vma=False)
```

profile of v0, /device:TPU:0, one launch (start us, length us, event | category | flops | bytes accessed | tf_op | source)
XLA Modules:
  0.0 384.4 jit_solution(9080420248376913407)
XLA Ops:
  6.5 8.5 %copy.3 = bf16[1,32768,64]{2,1,0:T(8,128)(2,1)} copy(bf16[1,32768,64]{1,2,0:T(8,128)(2,1)} %param.5) | data formatting | bytes 8388608 | tf_op args[0]
  15.0 31.2 %fusion.1 = f32[320,320]{1,0:T(8,128)} fusion(bf16[32768,256]{1,0:T(8,128)(2,1)} %bitcast.173, bf16[32768,64]{1,0:T(8,128)(2,1)} %bitcast.171), kind=kOutput, calls=%fused_computation.3 | convolution fusion | flops 6752829440 | bytes 21381120 | tf_op jit(solution)/shard_map/dot_general | solution.py:49
  46.4 75.3 %all-reduce.2.cloned.1.call-done = f32[320,320]{1,0:T(8,128)} async-done(((f32[320,320]{1,0:T(8,128)}), f32[320,320]{1,0:T(8,128)}) %all-reduce.2.cloned.1.call-update) | async-done | bytes 409616 | tf_op jit(solution)/shard_map/psum | solution.py:49
  124.1 5.8 %cholesky.164 = f32[64,64]{1,0:T(8,128)S(1)} custom-call(f32[64,64]{1,0:T(8,128)S(1)} %fusion.71), custom_call_target="Cholesky" | custom-call | tf_op jit(solution)/shard_map/jit(cholesky)/cholesky | solution.py:26
  131.3 4.9 %custom-call.14 = f32[1,64,64]{1,2,0:T(8,128)S(1)} custom-call(f32[1,64,64]{2,1,0:T(8,128)S(1)} %fusion.22), custom_call_target="InvertDiagBlocksLowerTriangular" | custom-call | tf_op jit(solution)/shard_map/jit(_solve_triangular)/triangular_solve | solution.py:27
  137.0 5.8 %cholesky.175 = f32[64,64]{1,0:T(8,128)S(1)} custom-call(f32[64,64]{1,0:T(8,128)S(1)} %fusion.67), custom_call_target="Cholesky" | custom-call | tf_op jit(solution)/shard_map/jit(cholesky)/cholesky | solution.py:26
  144.2 4.9 %custom-call.15 = f32[1,64,64]{1,2,0:T(8,128)S(1)} custom-call(f32[1,64,64]{2,1,0:T(8,128)S(1)} %fusion.23), custom_call_target="InvertDiagBlocksLowerTriangular" | custom-call | tf_op jit(solution)/shard_map/jit(_solve_triangular)/triangular_solve | solution.py:27
  149.7 1.6 fusion.13
  152.1 5.8 %cholesky.186 = f32[64,64]{1,0:T(8,128)S(1)} custom-call(f32[64,64]{1,0:T(8,128)S(1)} %fusion.63), custom_call_target="Cholesky" | custom-call | tf_op jit(solution)/shard_map/jit(cholesky)/cholesky | solution.py:26
  159.3 4.9 %custom-call.16 = f32[1,64,64]{1,2,0:T(8,128)S(1)} custom-call(f32[1,64,64]{2,1,0:T(8,128)S(1)} %fusion.24), custom_call_target="InvertDiagBlocksLowerTriangular" | custom-call | tf_op jit(solution)/shard_map/jit(_solve_triangular)/triangular_solve | solution.py:27
  165.0 5.8 %cholesky.197 = f32[64,64]{1,0:T(8,128)S(1)} custom-call(f32[64,64]{1,0:T(8,128)S(1)} %fusion.59), custom_call_target="Cholesky" | custom-call | tf_op jit(solution)/shard_map/jit(cholesky)/cholesky | solution.py:26
  172.2 4.9 %custom-call.17 = f32[1,64,64]{1,2,0:T(8,128)S(1)} custom-call(f32[1,64,64]{2,1,0:T(8,128)S(1)} %fusion.25), custom_call_target="InvertDiagBlocksLowerTriangular" | custom-call | tf_op jit(solution)/shard_map/jit(_solve_triangular)/triangular_solve | solution.py:27
  177.6 1.6 fusion.10
  180.1 6.0 %cholesky.208 = f32[64,64]{1,0:T(8,128)S(1)} custom-call(f32[64,64]{1,0:T(8,128)S(1)} %fusion.55), custom_call_target="Cholesky" | custom-call | tf_op jit(solution)/shard_map/jit(cholesky)/cholesky | solution.py:26
  187.4 4.9 %custom-call.18 = f32[1,64,64]{1,2,0:T(8,128)S(1)} custom-call(f32[1,64,64]{2,1,0:T(8,128)S(1)} %fusion.26), custom_call_target="InvertDiagBlocksLowerTriangular" | custom-call | tf_op jit(solution)/shard_map/jit(_solve_triangular)/triangular_solve | solution.py:27
  193.1 5.8 %cholesky.219 = f32[64,64]{1,0:T(8,128)S(1)} custom-call(f32[64,64]{1,0:T(8,128)S(1)} %fusion.51), custom_call_target="Cholesky" | custom-call | tf_op jit(solution)/shard_map/jit(cholesky)/cholesky | solution.py:26
  200.3 4.9 %custom-call.19 = f32[1,64,64]{1,2,0:T(8,128)S(1)} custom-call(f32[1,64,64]{2,1,0:T(8,128)S(1)} %fusion.27), custom_call_target="InvertDiagBlocksLowerTriangular" | custom-call | tf_op jit(solution)/shard_map/jit(_solve_triangular)/triangular_solve | solution.py:27
  205.7 1.6 fusion.7
  208.2 5.8 %cholesky.230 = f32[64,64]{1,0:T(8,128)S(1)} custom-call(f32[64,64]{1,0:T(8,128)S(1)} %fusion.47), custom_call_target="Cholesky" | custom-call | tf_op jit(solution)/shard_map/jit(cholesky)/cholesky | solution.py:26
  215.3 4.9 %custom-call.20 = f32[1,64,64]{1,2,0:T(8,128)S(1)} custom-call(f32[1,64,64]{2,1,0:T(8,128)S(1)} %fusion.28), custom_call_target="InvertDiagBlocksLowerTriangular" | custom-call | tf_op jit(solution)/shard_map/jit(_solve_triangular)/triangular_solve | solution.py:27
  221.0 5.8 %cholesky.241 = f32[64,64]{1,0:T(8,128)S(1)} custom-call(f32[64,64]{1,0:T(8,128)S(1)} %fusion.43), custom_call_target="Cholesky" | custom-call | tf_op jit(solution)/shard_map/jit(cholesky)/cholesky | solution.py:26
  228.2 4.9 %custom-call.21 = f32[1,64,64]{1,2,0:T(8,128)S(1)} custom-call(f32[1,64,64]{2,1,0:T(8,128)S(1)} %fusion.29), custom_call_target="InvertDiagBlocksLowerTriangular" | custom-call | tf_op jit(solution)/shard_map/jit(_solve_triangular)/triangular_solve | solution.py:27
  233.9 28.9 %fusion.90 = (bf16[32768,64]{0,1:T(8,128)(2,1)}, f32[32768,64]{0,1:T(8,128)}) fusion(f32[320,64]{1,0:T(8,128)S(1)} %fusion.5, bf16[32768,256]{1,0:T(8,128)(2,1)} %bitcast.174, bf16[32768,64]{1,0:T(8,128)(2,1)} %bitcast.172), kind=kOutput, calls=%fused_computation.150 | convolution fusion | flops 8097103872 | bytes 33636352 | tf_op jit(solution)/shard_map/dot_general | solution.py:32
  262.7 7.5 %collective-permute-done = bf16[32768,64]{0,1:T(8,128)(2,1)} collective-permute-done((bf16[32768,64]{0,1:T(8,128)(2,1)}, bf16[32768,64]{0,1:T(8,128)(2,1)}, u32[]{:S(2)}, u32[]{:S(2)}) %collective-permute-start) | collective-permute-done | bytes 4194336 | tf_op jit(solution)/shard_map/ppermute | solution.py:17
  270.2 12.1 %convert_select_fusion.1 = (f32[32768,64]{0,1:T(8,128)}, f32[32768,64]{0,1:T(8,128)}) fusion(f32[32768,64]{0,1:T(8,128)} %get-tuple-element.10, bf16[32768,64]{0,1:T(8,128)(2,1)} %collective-permute-done, pred[]{:T(512)S(6)} %eq.34), kind=kLoop, calls=%fused_computation.7 | loop fusion | flops 6291456 | bytes 29360128 | tf_op jit(solution)/shard_map/jit(_where)/select_n | solution.py:62
  282.3 18.3 %fusion.4 = bf16[128,128]{1,0:T(8,128)(2,1)S(1)} fusion(f32[32768,64]{0,1:T(8,128)} %get-tuple-element.8, f32[32768,64]{0,1:T(8,128)} %get-tuple-element.6), kind=kOutput, calls=%fused_computation.9 | convolution fusion | flops 6446661632 | bytes 16809984 | tf_op jit(solution)/shard_map/dot_general | solution.py:38
  300.7 35.5 %psum.15 = bf16[128,128]{1,0:T(8,128)(2,1)S(1)} all-reduce(bf16[128,128]{1,0:T(8,128)(2,1)S(1)} %fusion.4), channel_id=1, replica_groups=mesh['job'=2,'tm'=2,'rows'=8] {'rows'}, use_global_device_ids=true, to_apply=%region_3.6 | all-reduce | flops 16384 | bytes 65536 | tf_op jit(solution)/shard_map/psum | solution.py:65
  336.6 5.8 %cholesky.252 = f32[64,64]{1,0:T(8,128)S(1)} custom-call(f32[64,64]{1,0:T(8,128)S(1)} %fusion.39), custom_call_target="Cholesky" | custom-call | tf_op jit(solution)/shard_map/jit(cholesky)/cholesky | solution.py:26
  343.8 4.9 %custom-call.22 = f32[1,64,64]{1,2,0:T(8,128)S(1)} custom-call(f32[1,64,64]{2,1,0:T(8,128)S(1)} %fusion.30), custom_call_target="InvertDiagBlocksLowerTriangular" | custom-call | tf_op jit(solution)/shard_map/jit(_solve_triangular)/triangular_solve | solution.py:27
  349.5 5.8 %cholesky.263 = f32[64,64]{1,0:T(8,128)S(1)} custom-call(f32[64,64]{1,0:T(8,128)S(1)} %fusion.35), custom_call_target="Cholesky" | custom-call | tf_op jit(solution)/shard_map/jit(cholesky)/cholesky | solution.py:26
  356.6 4.9 %custom-call.23 = f32[1,64,64]{1,2,0:T(8,128)S(1)} custom-call(f32[1,64,64]{2,1,0:T(8,128)S(1)} %fusion.31), custom_call_target="InvertDiagBlocksLowerTriangular" | custom-call | tf_op jit(solution)/shard_map/jit(_solve_triangular)/triangular_solve | solution.py:27
  361.8 13.8 %fusion.2 = bf16[32768,64]{0,1:T(8,128)(2,1)S(1)} fusion(f32[64,128]{1,0:T(8,128)S(1)} %fusion.32, f32[32768,64]{0,1:T(8,128)} %get-tuple-element.8, f32[32768,64]{0,1:T(8,128)} %get-tuple-element.6), kind=kOutput, calls=%fused_computation.4 | convolution fusion | flops 3225419776 | bytes 21004288 | tf_op jit(solution)/shard_map/dot_general | solution.py:32
  (101 shorter events, 26.5 us)
Async XLA Ops:
  6.5 115.2 %all-reduce.2.cloned.1.call-start = ((), (), s32[]{:S(2)}) async-start(), calls=%async_computation | async-start | bytes 983040 | tf_op jit(solution)/shard_map/psum | solution.py:49
  262.7 7.5 %collective-permute-start = (bf16[32768,64]{0,1:T(8,128)(2,1)}, bf16[32768,64]{0,1:T(8,128)(2,1)}, u32[]{:S(2)}, u32[]{:S(2)}) collective-permute-start(bf16[32768,64]{0,1:T(8,128)(2,1)} %get-tuple-element.9), channel_id=1, source_target_pairs={{0,8},{8,0},{1,9},{9,1},{2,10},{10,2},{3,11},{11,3},{4,12},{12,4},... | collective-permute-start | bytes 12582920 | tf_op jit(solution)/shard_map/ppermute | solution.py:17
Sparse Core Ops, SparseCore 0:
  46.3 75.3 all-reduce.1
where the time goes:
time: 389 us; the launch traced here: 384 us
  other arithmetic  133 us (34%)
  matrix products  108 us (28%)
  waiting for transfers between devices  82.8 us (21%)
  blocking collectives  35.5 us (9%)
  between operations  14.4 us (4%)
  local copies, waits for them, and re-layouts  10.7 us (3%)
    psum x1, waiting for transfers between devices, shards(): lax.psum(jnp.dot(whole.T, whole, preferred_element_type=jnp.float32), 'ro...  75.3 us
    another operation x30, other arithmetic, basis_of(): lower = jnp.linalg.cholesky(inner)  65.3 us
    another operation x20, other arithmetic, basis_of(): basis = jax.scipy.linalg.solve_triangular(lower, image.T, lower=True).T  55.5 us
    dot_general x2, matrix products, project(): jnp.dot(joined, basis, precision=lax.Precision.HIGHEST, preferred_element...  42.7 us
    psum x1, blocking collectives, shards(): lax.psum(inner_rows(joined, joined).astype(jnp.bfloat16), 'rows')  35.5 us
    dot_general x1, matrix products, shards(): jnp.dot(whole.T, whole, preferred_element_type=jnp.float32)  31.2 us
    dot_general x1, matrix products, inner_rows(): jnp.dot(left.T, right, precision=lax.Precision.HIGHEST, preferred_element...  18.3 us
    select_n x1, other arithmetic, shards(): first = jnp.where(index == 0, modes, other)  12.1 us
  transfers between devices with their start and end apart: 2, of which 2 were waited for; matrix products, arithmetic and copies ran while one was open for 0% of the time, Pallas kernels for 0%

commit v1 on v0

v1 whole, which is shorter than its diff:
```python
import functools

import jax
import jax.numpy as jnp
from jax import lax
from jax.experimental import pallas as pl
from jax.experimental.pallas import tpu as pltpu
from jax.sharding import PartitionSpec as P

STEPS = 4
ITERS = 2
F32 = jnp.float32
NN = (((1,), (0,)), ((), ()))
NT = (((1,), (1,)), ((), ()))
TN = (((0,), (0,)), ((), ()))
VMEM = pltpu.MemorySpace.VMEM


def dot(a, b, dims=NN):
    return lax.dot_general(
        a, b, dims, precision=lax.Precision.HIGHEST, preferred_element_type=F32
    )


def fast(a, b, dims=NN):
    return lax.dot_general(a, b, dims, preferred_element_type=F32)


def spread_lanes(row):
    return jnp.broadcast_to(row, (8, row.shape[1]))


def spread_cols(col, width):
    return jnp.broadcast_to(col, (col.shape[0], width))


def iota(shape, dim):
    return lax.broadcasted_iota(jnp.int32, shape, dim)


def inverse_factor(square):
    order, width = square.shape
    lane = iota((order, width), 1)
    eye = (lane == iota((order, width), 0)).astype(F32)
    joined = jnp.where(lane < order, eye, square)
    rows = [joined[8 * b : 8 * b + 8] for b in range(order // 8)]
    sub = iota((8, width), 0)
    done = []
    for b in range(order // 8):
        here = rows[b]
        first = order + 8 * b
        cols = [spread_cols(here[:, first + j : first + j + 1], width) for j in range(8)]
        below = [
            [spread_cols(rows[t][:, first + j : first + j + 1], width) for j in range(8)]
            for t in range(b + 1, order // 8)
        ]
        kept = jnp.zeros_like(here)
        for j in range(8):
            pivot = spread_lanes(cols[j][j : j + 1])
            inv = 1.0 / pivot
            scaled = spread_lanes(here[j : j + 1]) * inv
            kept = jnp.where(sub == j, here * lax.rsqrt(pivot), kept)
            here = jnp.where(sub == j, scaled, here - cols[j] * scaled)
            for k in range(j + 1, 8):
                part = spread_lanes(cols[k][j : j + 1]) * inv
                cols[k] = jnp.where(sub == j, part, cols[k] - cols[j] * part)
        done.append(kept)
        if b + 1 < order // 8:
            flat = [spread_lanes(here[j : j + 1]) for j in range(8)]
            for at, t in enumerate(range(b + 1, order // 8)):
                terms = [below[at][j] * flat[j] for j in range(8)]
                while len(terms) > 1:
                    terms = [terms[i] + terms[i + 1] for i in range(0, len(terms), 2)]
                rows[t] = rows[t] - terms[0]
    full = jnp.concatenate(done, axis=0)
    return jnp.where(lane < order, full, 0.0)


def basis_rows(gram, keep):
    image = gram[:keep]
    for turn in range(ITERS):
        twice = jnp.concatenate([image, image], axis=0)
        inner = dot(image, twice, NT)
        basis = dot(inverse_factor(inner), twice)
        if turn + 1 < ITERS:
            image = dot(basis, gram)
    return basis


def unpack(packed, keep):
    tile = lambda i: packed[:, 128 * i : 128 * i + 128]
    lane = iota((keep, 128), 1)
    zero = jnp.zeros((keep, 128), F32)
    upper = jnp.concatenate(
        [
            jnp.concatenate([tile(0), tile(1)], axis=1),
            jnp.concatenate([tile(6), tile(2)], axis=1),
            jnp.concatenate([zero, tile(3)], axis=1),
            jnp.concatenate([zero, tile(7)], axis=1),
        ],
        axis=0,
    )
    size = upper.shape[0]
    row_block = iota((size, size), 0) // keep
    col_block = iota((size, size), 1) // keep
    square = jnp.where(row_block <= col_block, upper, upper.T)
    cross = jnp.concatenate([tile(4), tile(5)], axis=1)
    corner = jnp.where(lane < keep, tile(6), 0.0)
    low = jnp.concatenate([cross, corner], axis=1)
    cross_pad = jnp.concatenate([cross, jnp.zeros_like(cross)], axis=0)
    top = jnp.concatenate([square, cross_pad.T], axis=1)
    return jnp.concatenate([top, low, jnp.zeros_like(low)], axis=0)


def steps_kernel(left_ref, right_ref, out_ref, total_ref, weights_ref):
    keep = left_ref.shape[0]
    total_ref[...] = unpack(left_ref[...] + right_ref[...], keep)
    width = total_ref.shape[0]
    frames = STEPS * keep
    shape = (keep, width)
    weights_ref[...] = (iota(shape, 1) == iota(shape, 0) + frames).astype(F32)

    @pl.loop(0, STEPS)
    def _(step):
        picker = (iota(shape, 1) == iota(shape, 0) + step * keep).astype(F32)
        coeffs = jnp.concatenate([weights_ref[...], picker], axis=0)
        gram = dot(dot(coeffs, total_ref[...]), coeffs, NT)
        weights_ref[...] = dot(basis_rows(gram, keep), coeffs)

    out_ref[...] = weights_ref[...]


def steps_weights(left, right, keep):
    width = (STEPS + 2) * keep
    return pl.pallas_call(
        steps_kernel,
        out_shape=jax.ShapeDtypeStruct((keep, width), F32),
        in_specs=[pl.BlockSpec(memory_space=VMEM)] * 2,
        out_specs=pl.BlockSpec(memory_space=VMEM),
        scratch_shapes=[pltpu.VMEM((width, width), F32), pltpu.VMEM((keep, width), F32)],
        name="steps",
    )(left, right)


def gram_kernel(prior_ref, frames_ref, out_ref, square_ref, cross_ref, corner_ref):
    step = pl.program_id(0)

    @pl.when(step == 0)
    def _():
        square_ref[...] = jnp.zeros_like(square_ref)
        cross_ref[...] = jnp.zeros_like(cross_ref)
        corner_ref[...] = jnp.zeros_like(corner_ref)

    prior = prior_ref[...]
    frames = frames_ref[...]
    square_ref[...] += fast(frames, frames, TN)
    cross_ref[...] += fast(prior, frames)
    corner_ref[...] += fast(prior, prior, NT)

    @pl.when(step == pl.num_programs(0) - 1)
    def _():
        keep = prior_ref.shape[0]
        square = square_ref[...]
        corner = corner_ref[...]
        wide = jnp.concatenate([corner, jnp.zeros_like(corner)], axis=1)
        lane = iota(wide.shape, 1)
        out_ref[:, 0:256] = square[0:64]
        out_ref[:, 256:384] = square[64:128, 128:256]
        out_ref[:, 384:512] = square[128:192, 128:256]
        out_ref[:, 512:768] = cross_ref[...]
        out_ref[:, 768:896] = jnp.where(lane < keep, wide, square[64:128, 0:128])
        out_ref[:, 896:1024] = square[192:256, 128:256]


def local_gram(prior_t, frames, chunk):
    keep, rows = prior_t.shape
    width = frames.shape[1]
    return pl.pallas_call(
        gram_kernel,
        grid=(rows // chunk,),
        out_shape=jax.ShapeDtypeStruct((keep, 16 * keep), F32),
        in_specs=[
            pl.BlockSpec((keep, chunk), lambda i: (0, i)),
            pl.BlockSpec((chunk, width), lambda i: (i, 0)),
        ],
        out_specs=pl.BlockSpec((keep, 16 * keep), lambda i: (0, 0)),
        scratch_shapes=[
            pltpu.VMEM((width, width), F32),
            pltpu.VMEM((keep, width), F32),
            pltpu.VMEM((keep, keep), F32),
        ],
        name="gram",
    )(prior_t, frames)


def split(value):
    high = value.astype(jnp.bfloat16)
    return high, (value - high.astype(F32)).astype(jnp.bfloat16)


def modes_kernel(weights_ref, prior_ref, frames_ref, out_ref):
    keep = prior_ref.shape[0]
    width = frames_ref.shape[1]
    both = jnp.concatenate(split(weights_ref[...]), axis=0)
    part = fast(both[:, :width], frames_ref[...], NT)
    part += fast(both[:, width : width + keep], prior_ref[...])
    out_ref[...] = (part[:keep] + part[keep:]).astype(out_ref.dtype)


def project(weights, prior_t, frames, chunk, first, count):
    keep, rows = prior_t.shape
    width = frames.shape[1]
    return pl.pallas_call(
        modes_kernel,
        grid=(count,),
        out_shape=jax.ShapeDtypeStruct((keep, count * chunk), jnp.bfloat16),
        in_specs=[
            pl.BlockSpec(weights.shape, lambda i: (0, 0)),
            pl.BlockSpec((keep, chunk), lambda i: (0, i + first)),
            pl.BlockSpec((chunk, width), lambda i: (i + first, 0)),
        ],
        out_specs=pl.BlockSpec((keep, chunk), lambda i: (0, i)),
        name="project",
    )(weights, prior_t, frames)


def pair_kernel(own_ref, other_ref, out_ref):
    @pl.when(pl.program_id(0) == 0)
    def _():
        out_ref[...] = jnp.zeros_like(out_ref)

    both = jnp.concatenate([own_ref[...], other_ref[...]], axis=0)
    out_ref[...] += fast(both, both, NT)


def pair_gram(own, other, chunk):
    keep, rows = own.shape
    block = pl.BlockSpec((keep, chunk), lambda i: (0, i))
    return pl.pallas_call(
        pair_kernel,
        grid=(rows // chunk,),
        out_shape=jax.ShapeDtypeStruct((2 * keep, 2 * keep), F32),
        in_specs=[block, block],
        out_specs=pl.BlockSpec((2 * keep, 2 * keep), lambda i: (0, 0)),
        name="pair",
    )(own, other)


def merge_kernel(index_ref, left_ref, right_ref, out_ref):
    gram = left_ref[...] + right_ref[...]
    keep = gram.shape[0] // 2
    first = index_ref[0] == 0
    swapped = pltpu.roll(pltpu.roll(gram, keep, 1), keep, 0)
    basis = basis_rows(jnp.where(first, gram, swapped), keep)
    half = out_ref.shape[0]
    out_ref[...] = jnp.where(first, basis[:half], pltpu.roll(basis[half:], keep, 1))


def merge_weights(index, left, right):
    order = left.shape[0]
    return pl.pallas_call(
        merge_kernel,
        out_shape=jax.ShapeDtypeStruct((order // 4, order), F32),
        in_specs=[pl.BlockSpec(memory_space=pltpu.MemorySpace.SMEM)]
        + [pl.BlockSpec(memory_space=VMEM)] * 2,
        out_specs=pl.BlockSpec(memory_space=VMEM),
        name="merge",
    )(index, left, right)


def output_kernel(weights_ref, own_ref, other_ref, out_ref):
    half = out_ref.shape[0]
    both = jnp.concatenate([own_ref[...], other_ref[...]], axis=0)
    part = fast(jnp.concatenate(split(weights_ref[...]), axis=0), both)
    out_ref[...] = (part[:half] + part[half:]).astype(out_ref.dtype)


def output(weights, own, other, chunk):
    keep, rows = own.shape
    block = pl.BlockSpec((keep, chunk), lambda i: (0, i))
    return pl.pallas_call(
        output_kernel,
        grid=(rows // chunk,),
        out_shape=jax.ShapeDtypeStruct((keep // 2, rows), jnp.bfloat16),
        in_specs=[pl.BlockSpec(weights.shape, lambda i: (0, 0)), block, block],
        out_specs=pl.BlockSpec((keep // 2, chunk), lambda i: (0, i)),
        name="output",
    )(weights, own, other)


def flip(block, axis, mask):
    count = lax.axis_size(axis)
    return lax.ppermute(block, axis, [(i, i ^ mask) for i in range(count)])


def all_but_last_sum(value, axis):
    count = lax.axis_size(axis)
    mask = 1
    while 2 * mask < count:
        value = value + flip(value, axis, mask)
        mask *= 2
    return value, flip(value, axis, mask)


def block_of(rows, limit):
    size = min(rows, limit)
    while rows % size:
        size //= 2
    return size


def shards(prior, snapshots):
    prior_t = prior[0].T
    frames = snapshots[0]
    keep, rows = prior_t.shape
    local = local_gram(prior_t, frames, block_of(rows, 8192))
    weights = steps_weights(*all_but_last_sum(local, "rows"), keep)
    own = project(weights, prior_t, frames, block_of(rows, 4096), 0, rows // block_of(rows, 4096))
    other = flip(own, "tm", 1)
    gram = pair_gram(own, other, block_of(rows, 8192))
    index = lax.axis_index("tm").astype(jnp.int32).reshape(1)
    final = merge_weights(index, *all_but_last_sum(gram, "rows"))
    return output(final, own, other, block_of(rows, 8192)).T


def solution(mesh):
    in_specs = (P("tm", ("job", "rows"), None), P("tm", ("job", "rows"), None))
    out_specs = P(("job", "rows"), "tm")
    return jax.shard_map(shards, mesh=mesh, in_specs=in_specs, out_specs=out_specs, check_vma=False)
```

time: 389 us -> 129 us (0.33); the launches traced: 384 us -> 129 us
  other arithmetic: 133 us -> 1.88 us
  matrix products: 108 us -> 0 us
  Pallas kernels: 0 us -> 73 us
  waiting for transfers between devices: 82.8 us -> 41.8 us
  blocking collectives: 35.5 us -> 0 us
  between operations: 14.4 us -> 0.04 us
  starting transfers between devices: 0.01 us -> 10.7 us
  local copies, waits for them, and re-layouts: 10.7 us -> 1.34 us
    another operation x50 -> x0, other arithmetic: 121 us -> none  [the longest x30 65.3 us: basis_of(): lower = jnp.linalg.cholesky(inner)]
    dot_general x36 -> x0, matrix products: 105 us -> none  [the longest x2 42.7 us: project(): jnp.dot(joined, basis, precision=lax.Precision.HIGHEST, preferred_element...]
    psum x1 -> x0, waiting for transfers between devices: 75.3 us -> none  [shards(): lax.psum(jnp.dot(whole.T, whole, preferred_element_type=jnp.float32), 'ro...]
    pallas_call x0 -> x6, Pallas kernels: none -> 73 us  [the longest x1 27.4 us: steps_weights(): pl.pallas_call(steps_kernel, out_shape=jax.ShapeDtypeStruct((keep, width)...]
    psum x1 -> x0, blocking collectives: 35.5 us -> none  [shards(): lax.psum(inner_rows(joined, joined).astype(jnp.bfloat16), 'rows')]
    ppermute x1 -> x7, waiting for transfers between devices: 7.5 us -> 41.8 us  [flip(): return lax.ppermute(block, axis, [(i, i ^ mask) for i in range(count)])]
    select_n x1 -> x0, other arithmetic: 12.1 us -> none  [shards(): first = jnp.where(index == 0, modes, other)]
    ppermute x1 -> x7, starting transfers between devices: 0.01 us -> 10.7 us  [flip(): return lax.ppermute(block, axis, [(i, i ^ mask) for i in range(count)])]
  transfers between devices with their start and end apart: 2 -> 7, of which waited for: 2 -> 7; matrix products, arithmetic and copies ran while one was open for 0% -> 0% of each run, Pallas kernels for 0% -> 0%
where the time goes in v1:
time: 129 us
  Pallas kernels  73 us (57%)
  waiting for transfers between devices  41.8 us (32%)
  starting transfers between devices  10.7 us (8%)
  other arithmetic  1.88 us (1%)
  local copies, waits for them, and re-layouts  1.34 us (1%)
    ppermute x7, waiting for transfers between devices, flip(): return lax.ppermute(block, axis, [(i, i ^ mask) for i in range(count)])  41.8 us
    pallas_call x1, Pallas kernels, steps_weights(): pl.pallas_call(steps_kernel, out_shape=jax.ShapeDtypeStruct((keep, width)...  27.4 us
    pallas_call x1, Pallas kernels, project(): pl.pallas_call(modes_kernel, grid=(count,), out_shape=jax.ShapeDtypeStruc...  14.2 us
    pallas_call x1, Pallas kernels, local_gram(): pl.pallas_call(gram_kernel, grid=(rows // chunk,), out_shape=jax.ShapeDty...  12.7 us
    ppermute x7, starting transfers between devices, flip(): return lax.ppermute(block, axis, [(i, i ^ mask) for i in range(count)])  10.7 us
    pallas_call x1, Pallas kernels, merge_weights(): pl.pallas_call(merge_kernel, out_shape=jax.ShapeDtypeStruct((order // 4,...  6.87 us
    pallas_call x1, Pallas kernels, pair_gram(): pl.pallas_call(pair_kernel, grid=(rows // chunk,), out_shape=jax.ShapeDty...  6.04 us
    pallas_call x1, Pallas kernels, output(): pl.pallas_call(output_kernel, grid=(rows // chunk,), out_shape=jax.ShapeD...  5.85 us
  transfers between devices with their start and end apart: 7, of which 7 were waited for; matrix products, arithmetic and copies ran while one was open for 0% of the time, Pallas kernels for 0%

profile of v1, /device:TPU:0, one launch (start us, length us, event | category | flops | bytes accessed | tf_op | source)
XLA Modules:
  0.0 128.8 jit_solution(8010594476907663938)
XLA Ops:
  0.0 12.7 %gram.1 = f32[64,1024]{1,0:T(8,128)} custom-call(bf16[64,32768]{1,0:T(8,128)(2,1)} %bitcast.8, bf16[32768,256]{1,0:T(8,128)(2,1)} %bitcast.6), custom_call_target="tpu_custom_call" | custom-call | tf_op jit(solution)/shard_map/gram/pallas_call | solution.py:178
  12.7 3.0 %collective-permute-start = (f32[64,1024]{1,0:T(8,128)}, f32[64,1024]{1,0:T(8,128)S(1)}, u32[]{:S(2)}, u32[]{:S(2)}) collective-permute-start(f32[64,1024]{1,0:T(8,128)} %gram.1), channel_id=1, source_target_pairs={{0,1},{1,0},{2,3},{3,2},{4,5},{5,4},{6,7},{7,6},{8,9},{9,8},{10,11... | collective-permute-start | bytes 786440 | tf_op jit(solution)/shard_map/ppermute | solution.py:293
  15.7 6.5 %collective-permute-done = f32[64,1024]{1,0:T(8,128)S(1)} collective-permute-done((f32[64,1024]{1,0:T(8,128)}, f32[64,1024]{1,0:T(8,128)S(1)}, u32[]{:S(2)}, u32[]{:S(2)}) %collective-permute-start) | collective-permute-done | bytes 262176 | tf_op jit(solution)/shard_map/ppermute | solution.py:293
  22.2 1.0 add.12
  23.2 1.8 %collective-permute-start.1 = (f32[64,1024]{1,0:T(8,128)S(1)}, f32[64,1024]{1,0:T(8,128)S(1)}, u32[]{:S(2)}, u32[]{:S(2)}) collective-permute-start(f32[64,1024]{1,0:T(8,128)S(1)} %add.12), channel_id=1, source_target_pairs={{0,2},{1,3},{2,0},{3,1},{4,6},{5,7},{6,4},{7,5},{8,10},{9,11},{10,... | collective-permute-start | bytes 786440 | tf_op jit(solution)/shard_map/ppermute | solution.py:293
  25.0 5.7 %collective-permute-done.1 = f32[64,1024]{1,0:T(8,128)S(1)} collective-permute-done((f32[64,1024]{1,0:T(8,128)S(1)}, f32[64,1024]{1,0:T(8,128)S(1)}, u32[]{:S(2)}, u32[]{:S(2)}) %collective-permute-start.1) | collective-permute-done | bytes 262176 | tf_op jit(solution)/shard_map/ppermute | solution.py:293
  30.8 0.0 copy-start
  30.8 2.6 %collective-permute-start.2 = (f32[64,1024]{1,0:T(8,128)S(1)}, f32[64,1024]{1,0:T(8,128)S(1)}, u32[]{:S(2)}, u32[]{:S(2)}) collective-permute-start(f32[64,1024]{1,0:T(8,128)S(1)} %add.13.left_ref), channel_id=1, source_target_pairs={{0,4},{1,5},{2,6},{3,7},{4,0},{5,1},{6,2},{7,3},{8,12},{9,13},{10,... | collective-permute-start | bytes 786440 | tf_op jit(solution)/shard_map/ppermute | solution.py:293
  33.4 10.6 %collective-permute-done.2.right_ref = f32[64,1024]{1,0:T(8,128)S(1)} collective-permute-done((f32[64,1024]{1,0:T(8,128)S(1)}, f32[64,1024]{1,0:T(8,128)S(1)}, u32[]{:S(2)}, u32[]{:S(2)}) %collective-permute-start.2) | collective-permute-done | bytes 262176 | tf_op jit(solution)/shard_map/ppermute | solution.py:293
  44.0 0.0 copy-done
  44.0 0.0 copy-start.2
  44.0 0.7 copy-done.2
  44.7 27.4 %steps.1.weights_ref = f32[64,384]{1,0:T(8,128)} custom-call(f32[64,1024]{1,0:T(8,128)} %copy-done, f32[64,1024]{1,0:T(8,128)} %copy-done.2), custom_call_target="tpu_custom_call" | custom-call | tf_op jit(solution)/shard_map/steps/pallas_call | solution.py:135
  72.1 14.2 %project.1.own_ref = bf16[64,32768]{1,0:T(8,128)(2,1)} custom-call(f32[64,384]{1,0:T(8,128)} %steps.1.weights_ref, bf16[64,32768]{1,0:T(8,128)(2,1)} %bitcast.9, bf16[32768,256]{1,0:T(8,128)(2,1)} %bitcast.7), custom_call_target="tpu_custom_call" | custom-call | tf_op jit(solution)/shard_map/project/pallas_call | solution.py:213
  86.3 0.0 collective-permute-start.3
  86.3 7.5 %collective-permute-done.3.other_ref = bf16[64,32768]{1,0:T(8,128)(2,1)} collective-permute-done((bf16[64,32768]{1,0:T(8,128)(2,1)}, bf16[64,32768]{1,0:T(8,128)(2,1)}, u32[]{:S(2)}, u32[]{:S(2)}) %collective-permute-start.3) | collective-permute-done | bytes 4194336 | tf_op jit(solution)/shard_map/ppermute | solution.py:293
  93.8 6.0 %pair.1 = f32[128,128]{1,0:T(8,128)} custom-call(bf16[64,32768]{1,0:T(8,128)(2,1)} %project.1.own_ref, bf16[64,32768]{1,0:T(8,128)(2,1)} %collective-permute-done.3.other_ref), custom_call_target="tpu_custom_call" | custom-call | tf_op jit(solution)/shard_map/pair/pallas_call | solution.py:239
  99.8 1.2 collective-permute-start.4
  101.0 3.3 %collective-permute-done.4 = f32[128,128]{1,0:T(8,128)S(1)} collective-permute-done((f32[128,128]{1,0:T(8,128)}, f32[128,128]{1,0:T(8,128)S(1)}, u32[]{:S(2)}, u32[]{:S(2)}) %collective-permute-start.4) | collective-permute-done | bytes 65568 | tf_op jit(solution)/shard_map/ppermute | solution.py:293
  104.3 0.9 add.14
  105.2 0.3 collective-permute-start.5
  105.5 4.0 %collective-permute-done.5 = f32[128,128]{1,0:T(8,128)S(1)} collective-permute-done((f32[128,128]{1,0:T(8,128)S(1)}, f32[128,128]{1,0:T(8,128)S(1)}, u32[]{:S(2)}, u32[]{:S(2)}) %collective-permute-start.5) | collective-permute-done | bytes 65568 | tf_op jit(solution)/shard_map/ppermute | solution.py:293
  109.5 0.0 copy-start.1
  109.5 1.7 %collective-permute-start.6 = (f32[128,128]{1,0:T(8,128)S(1)}, f32[128,128]{1,0:T(8,128)S(1)}, u32[]{:S(2)}, u32[]{:S(2)}) collective-permute-start(f32[128,128]{1,0:T(8,128)S(1)} %add.15.left_ref), channel_id=1, source_target_pairs={{0,4},{1,5},{2,6},{3,7},{4,0},{5,1},{6,2},{7,3},{8,12},{9,13},{10,... | collective-permute-start | bytes 196616 | tf_op jit(solution)/shard_map/ppermute | solution.py:293
  111.2 4.2 %collective-permute-done.6.right_ref = f32[128,128]{1,0:T(8,128)S(1)} collective-permute-done((f32[128,128]{1,0:T(8,128)S(1)}, f32[128,128]{1,0:T(8,128)S(1)}, u32[]{:S(2)}, u32[]{:S(2)}) %collective-permute-start.6) | collective-permute-done | bytes 65568 | tf_op jit(solution)/shard_map/ppermute | solution.py:293
  115.4 0.0 copy-start.3
  115.4 0.0 copy-done.1
  115.4 0.6 copy-done.3
  116.1 6.9 %merge.1.weights_ref = f32[32,128]{1,0:T(8,128)} custom-call(s32[1]{0:T(128)} %bitcast.index_ref, f32[128,128]{1,0:T(8,128)} %copy-done.1, f32[128,128]{1,0:T(8,128)} %copy-done.3), custom_call_target="tpu_custom_call" | custom-call | tf_op jit(solution)/shard_map/merge/pallas_call | solution.py:261
  122.9 5.9 %output.1 = bf16[32,32768]{1,0:T(8,128)(2,1)} custom-call(f32[32,128]{1,0:T(8,128)} %merge.1.weights_ref, bf16[64,32768]{1,0:T(8,128)(2,1)} %project.1.own_ref, bf16[64,32768]{1,0:T(8,128)(2,1)} %collective-permute-done.3.other_ref), custom_call_target="tpu_custom_call" | custom-call | tf_op jit(solution)/shard_map/output/pallas_call | solution.py:281
  (2 shorter events, 0.0 us)
Async XLA Ops:
  12.7 9.5 %collective-permute-start = (f32[64,1024]{1,0:T(8,128)}, f32[64,1024]{1,0:T(8,128)S(1)}, u32[]{:S(2)}, u32[]{:S(2)}) collective-permute-start(f32[64,1024]{1,0:T(8,128)} %gram.1), channel_id=1, source_target_pairs={{0,1},{1,0},{2,3},{3,2},{4,5},{5,4},{6,7},{7,6},{8,9},{9,8},{10,11... | collective-permute-start | bytes 786440 | tf_op jit(solution)/shard_map/ppermute | solution.py:293
  23.2 7.5 %collective-permute-start.1 = (f32[64,1024]{1,0:T(8,128)S(1)}, f32[64,1024]{1,0:T(8,128)S(1)}, u32[]{:S(2)}, u32[]{:S(2)}) collective-permute-start(f32[64,1024]{1,0:T(8,128)S(1)} %add.12), channel_id=1, source_target_pairs={{0,2},{1,3},{2,0},{3,1},{4,6},{5,7},{6,4},{7,5},{8,10},{9,11},{10,... | collective-permute-start | bytes 786440 | tf_op jit(solution)/shard_map/ppermute | solution.py:293
  30.8 13.2 %copy-start = (f32[64,1024]{1,0:T(8,128)}, f32[64,1024]{1,0:T(8,128)S(1)}, u32[]{:S(2)}) copy-start(f32[64,1024]{1,0:T(8,128)S(1)} %add.13.left_ref) | copy-start | bytes 786436
  30.8 13.2 %collective-permute-start.2 = (f32[64,1024]{1,0:T(8,128)S(1)}, f32[64,1024]{1,0:T(8,128)S(1)}, u32[]{:S(2)}, u32[]{:S(2)}) collective-permute-start(f32[64,1024]{1,0:T(8,128)S(1)} %add.13.left_ref), channel_id=1, source_target_pairs={{0,4},{1,5},{2,6},{3,7},{4,0},{5,1},{6,2},{7,3},{8,12},{9,13},{10,... | collective-permute-start | bytes 786440 | tf_op jit(solution)/shard_map/ppermute | solution.py:293
  44.0 0.7 copy-start.2
  86.3 7.5 %collective-permute-start.3 = (bf16[64,32768]{1,0:T(8,128)(2,1)}, bf16[64,32768]{1,0:T(8,128)(2,1)}, u32[]{:S(2)}, u32[]{:S(2)}) collective-permute-start(bf16[64,32768]{1,0:T(8,128)(2,1)} %project.1.own_ref), channel_id=1, source_target_pairs={{0,8},{8,0},{1,9},{9,1},{2,10},{10,2},{3,11},{11,3},{4,12},{12,4},... | collective-permute-start | bytes 12582920 | tf_op jit(solution)/shard_map/ppermute | solution.py:293
  99.8 4.5 %collective-permute-start.4 = (f32[128,128]{1,0:T(8,128)}, f32[128,128]{1,0:T(8,128)S(1)}, u32[]{:S(2)}, u32[]{:S(2)}) collective-permute-start(f32[128,128]{1,0:T(8,128)} %pair.1), channel_id=1, source_target_pairs={{0,1},{1,0},{2,3},{3,2},{4,5},{5,4},{6,7},{7,6},{8,9},{9,8},{10,11... | collective-permute-start | bytes 196616 | tf_op jit(solution)/shard_map/ppermute | solution.py:293
  105.2 4.3 %collective-permute-start.5 = (f32[128,128]{1,0:T(8,128)S(1)}, f32[128,128]{1,0:T(8,128)S(1)}, u32[]{:S(2)}, u32[]{:S(2)}) collective-permute-start(f32[128,128]{1,0:T(8,128)S(1)} %add.14), channel_id=1, source_target_pairs={{0,2},{1,3},{2,0},{3,1},{4,6},{5,7},{6,4},{7,5},{8,10},{9,11},{10,... | collective-permute-start | bytes 196616 | tf_op jit(solution)/shard_map/ppermute | solution.py:293
  109.5 5.9 %copy-start.1 = (f32[128,128]{1,0:T(8,128)}, f32[128,128]{1,0:T(8,128)S(1)}, u32[]{:S(2)}) copy-start(f32[128,128]{1,0:T(8,128)S(1)} %add.15.left_ref) | copy-start | bytes 196612
  109.5 5.9 %collective-permute-start.6 = (f32[128,128]{1,0:T(8,128)S(1)}, f32[128,128]{1,0:T(8,128)S(1)}, u32[]{:S(2)}, u32[]{:S(2)}) collective-permute-start(f32[128,128]{1,0:T(8,128)S(1)} %add.15.left_ref), channel_id=1, source_target_pairs={{0,4},{1,5},{2,6},{3,7},{4,0},{5,1},{6,2},{7,3},{8,12},{9,13},{10,... | collective-permute-start | bytes 196616 | tf_op jit(solution)/shard_map/ppermute | solution.py:293
  115.4 0.6 copy-start.3

commit v2 on v1

v2 whole, which is shorter than its diff:
```python
import functools

import jax
import jax.numpy as jnp
from jax import lax
from jax.experimental import pallas as pl
from jax.experimental.pallas import tpu as pltpu
from jax.sharding import PartitionSpec as P

STEPS = 4
ITERS = 2
F32 = jnp.float32
NN = (((1,), (0,)), ((), ()))
NT = (((1,), (1,)), ((), ()))
TN = (((0,), (0,)), ((), ()))
VMEM = pltpu.MemorySpace.VMEM
PIECES = 4
CHUNK = 4096
GRAM_MB, PROJ_MB, PAIR_MB, OUT_MB = 36, 12, 6, 8
OUTVM = pltpu.VMEM


def dot(a, b, dims=NN):
    return lax.dot_general(
        a, b, dims, precision=lax.Precision.HIGHEST, preferred_element_type=F32
    )


def fast(a, b, dims=NN):
    return lax.dot_general(a, b, dims, preferred_element_type=F32)


def spread_lanes(row):
    return jnp.broadcast_to(row, (8, row.shape[1]))


def spread_cols(col, width):
    return jnp.broadcast_to(col, (col.shape[0], width))


def grant(mebibytes):
    return pltpu.CompilerParams(vmem_limit_bytes=mebibytes << 20)


def iota(shape, dim):
    return lax.broadcasted_iota(jnp.int32, shape, dim)


def pair_sum(terms):
    while len(terms) > 1:
        terms = [a + b for a, b in zip(terms[::2], terms[1::2])]
    return terms[0]


def inverse_factor(square, zero):
    order, width = square.shape
    lane = iota((order, width), 1)
    eye = (lane == iota((order, width), 0)).astype(F32)
    joined = jnp.where(lane < order, eye, square)
    count = order // 8
    rows = [joined[8 * b : 8 * b + 8] for b in range(count)]
    sub = iota((8, width), 0)
    done = []
    for b in range(count):
        here = rows[b]
        first = order + 8 * b
        cols = [spread_cols(here[:, first + j : first + j + 1], width) + zero for j in range(8)]
        below = [
            [spread_cols(rows[t][:, first + j : first + j + 1], width) for t in range(b + 1, count)]
            for j in range(8)
        ]
        kept = here
        for j in range(0, 8, 2):
            left, right = cols[j], cols[j + 1]
            at_left, at_right = sub == j, sub == j + 1
            pp, pq, qq = (
                spread_lanes(left[j : j + 1]),
                spread_lanes(right[j : j + 1]),
                spread_lanes(right[j + 1 : j + 2]),
            )
            inv = 1.0 / (pp * qq - pq * pq)
            ipp, ipq, iqq = qq * inv, -pq * inv, pp * inv

            def solve(value):
                top, low = spread_lanes(value[j : j + 1]), spread_lanes(value[j + 1 : j + 2])
                up, down = ipp * top + ipq * low, ipq * top + iqq * low
                rest = value - (left * up + right * down)
                return top, low, jnp.where(at_left, up, jnp.where(at_right, down, rest))

            for k in range(j + 2, 8):
                cols[k] = solve(cols[k])[2]
            top, low, here = solve(here)
            scale = lax.rsqrt(pp)
            ratio = pq * scale
            unit = top * scale
            kept = jnp.where(at_left, unit, kept)
            kept = jnp.where(
                at_right, (low - ratio * unit) * lax.rsqrt(qq - ratio * ratio), kept
            )
        done.append(kept)
        if b + 1 < count:
            flat = [spread_lanes(here[j : j + 1]) for j in range(8)]
            for t in range(b + 1, count):
                rows[t] = rows[t] - pair_sum([below[j][t - b - 1] * flat[j] for j in range(8)])
    return jnp.where(lane < order, jnp.concatenate(done, axis=0), 0.0)


def basis_rows(gram, keep, zero):
    image = gram[:keep]
    for turn in range(ITERS):
        twice = jnp.concatenate([image, image], axis=0)
        inner = dot(image, twice, NT)
        basis = dot(inverse_factor(inner, zero), twice)
        if turn + 1 < ITERS:
            image = dot(basis, gram)
    return basis


def unpack(packed, keep):
    tile = lambda i: packed[:, 128 * i : 128 * i + 128]
    lane = iota((keep, 128), 1)
    zero = jnp.zeros((keep, 128), F32)
    upper = jnp.concatenate(
        [
            jnp.concatenate([tile(0), tile(1)], axis=1),
            jnp.concatenate([tile(6), tile(2)], axis=1),
            jnp.concatenate([zero, tile(3)], axis=1),
            jnp.concatenate([zero, tile(7)], axis=1),
        ],
        axis=0,
    )
    size = upper.shape[0]
    row_block = iota((size, size), 0) // keep
    col_block = iota((size, size), 1) // keep
    square = jnp.where(row_block <= col_block, upper, upper.T)
    cross = jnp.concatenate([tile(4), tile(5)], axis=1)
    corner = jnp.where(lane < keep, tile(6), 0.0)
    low = jnp.concatenate([cross, corner], axis=1)
    cross_pad = jnp.concatenate([cross, jnp.zeros_like(cross)], axis=0)
    top = jnp.concatenate([square, cross_pad.T], axis=1)
    return jnp.concatenate([top, low, jnp.zeros_like(low)], axis=0)


def unit_trace(gram):
    eye = iota(gram.shape, 0) == iota(gram.shape, 1)
    return gram / jnp.sum(jnp.where(eye, gram, 0.0))


def steps_kernel(left_ref, right_ref, out_ref, total_ref, both_ref, zero_ref):
    keep = left_ref.shape[0]
    zero_ref[...] = jnp.zeros_like(zero_ref)
    total = unit_trace(unpack(left_ref[...] + right_ref[...], keep))
    total_ref[...] = total
    width = total.shape[0]
    frames = STEPS * keep
    shape = (keep, width)
    both_ref[:keep, :width] = total[frames : frames + keep]
    both_ref[:keep, width:] = (iota(shape, 1) == iota(shape, 0) + frames).astype(F32)

    @pl.loop(0, STEPS)
    def _(step):
        at = pl.multiple_of(step * keep, keep)
        both_ref[keep:, :width] = total_ref[pl.ds(at, keep)]
        both_ref[keep:, width:] = (iota(shape, 1) == iota(shape, 0) + at).astype(F32)
        both = both_ref[...]
        gram = dot(both[:, :width], both[:, width:], NT)
        both_ref[:keep] = dot(basis_rows(gram, keep, zero_ref[...]), both)

    out_ref[...] = both_ref[:keep, width:]


def steps_weights(left, right, keep):
    width = (STEPS + 2) * keep
    return pl.pallas_call(
        steps_kernel,
        out_shape=jax.ShapeDtypeStruct((keep, width), F32),
        in_specs=[pl.BlockSpec(memory_space=VMEM)] * 2,
        out_specs=pl.BlockSpec(memory_space=VMEM),
        scratch_shapes=[
            pltpu.VMEM((width, width), F32),
            pltpu.VMEM((2 * keep, 2 * width), F32),
            pltpu.VMEM((8, 2 * keep), F32),
        ],
        name="steps",
        compiler_params=grant(6),
    )(left, right)


def gram_kernel(prior_in, frames_in, out_ref, prior_ref, frames_ref, sems, square_ref, corner_ref):
    keep, rows = prior_ref.shape
    width = frames_ref.shape[1]
    count = sems.shape[1]
    size = rows // count

    def copies(i):
        at = slice(i * size, i * size + size)
        return (
            pltpu.make_async_copy(prior_in.at[:, at], prior_ref.at[:, at], sems.at[0, i]),
            pltpu.make_async_copy(frames_in.at[at], frames_ref.at[at], sems.at[1, i]),
        )

    for i in range(count):
        for copy in copies(i):
            copy.start()
    for i in range(count):
        for copy in copies(i):
            copy.wait()
        at = slice(i * size, i * size + size)
        frames = frames_ref[at]
        prior = prior_ref[:, at]
        part = fast(jnp.concatenate([frames.T, prior], axis=0), frames)
        last = fast(prior, prior, NT)
        square_ref[...] = part if i == 0 else square_ref[...] + part
        corner_ref[...] = last if i == 0 else corner_ref[...] + last

    corner = corner_ref[...]
    wide = jnp.concatenate([corner, jnp.zeros_like(corner)], axis=1)
    lane = iota(wide.shape, 1)
    out_ref[:, 0:256] = square_ref[0:64]
    out_ref[:, 256:384] = square_ref[64:128, 128:256]
    out_ref[:, 384:512] = square_ref[128:192, 128:256]
    out_ref[:, 512:768] = square_ref[256:320]
    out_ref[:, 768:896] = jnp.where(lane < keep, wide, square_ref[64:128, 0:128])
    out_ref[:, 896:1024] = square_ref[192:256, 128:256]


def local_gram(prior_t, frames, size):
    keep, rows = prior_t.shape
    width = frames.shape[1]
    return pl.pallas_call(
        gram_kernel,
        out_shape=(
            jax.ShapeDtypeStruct((keep, 16 * keep), F32),
            OUTVM(prior_t.shape, prior_t.dtype),
            OUTVM(frames.shape, frames.dtype),
        ),
        in_specs=[pl.BlockSpec(memory_space=pltpu.MemorySpace.HBM)] * 2,
        out_specs=[pl.BlockSpec(memory_space=VMEM)] * 3,
        scratch_shapes=[
            pltpu.SemaphoreType.DMA((2, rows // size)),
            pltpu.VMEM((width + keep, width), F32),
            pltpu.VMEM((keep, keep), F32),
        ],
        name="gram",
        compiler_params=grant(GRAM_MB),
    )(prior_t, frames)


def split(value):
    high = value.astype(jnp.bfloat16)
    return high, (value - high.astype(F32)).astype(jnp.bfloat16)


def modes_kernel(first, weights_ref, prior_ref, frames_ref, out_ref):
    keep = prior_ref.shape[0]
    width = frames_ref.shape[1]
    rows = out_ref.shape[1]
    both = jnp.concatenate(split(weights_ref[:, : width + keep]), axis=0)
    size = block_of(rows, 2048)
    for at in range(0, rows, size):
        here = slice(first + at, first + at + size)
        whole = jnp.concatenate([frames_ref[here].T, prior_ref[:, here]], axis=0)
        part = fast(both, whole)
        out_ref[:, at : at + size] = (part[:keep] + part[keep:]).astype(out_ref.dtype)


def project(weights, prior_t, frames, first, rows):
    keep = prior_t.shape[0]
    return pl.pallas_call(
        functools.partial(modes_kernel, first),
        out_shape=OUTVM((keep, rows), jnp.bfloat16),
        in_specs=[pl.BlockSpec(memory_space=VMEM)] * 3,
        out_specs=pl.BlockSpec(memory_space=VMEM),
        name="project",
        compiler_params=grant(PROJ_MB),
    )(weights, prior_t, frames)


def pair_kernel(own_ref, other_ref, *rest):
    out_ref = rest[-1]
    both = jnp.concatenate([own_ref[...], other_ref[...]], axis=0)
    gram = fast(both, both, NT)
    out_ref[...] = rest[0][...] + gram if len(rest) > 1 else gram


def pair_gram(own, other, *sofar):
    keep = own.shape[0]
    return pl.pallas_call(
        pair_kernel,
        out_shape=jax.ShapeDtypeStruct((2 * keep, 2 * keep), F32),
        in_specs=[pl.BlockSpec(memory_space=VMEM)] * (2 + len(sofar)),
        out_specs=pl.BlockSpec(memory_space=VMEM),
        name="pair",
        compiler_params=grant(PAIR_MB),
    )(own, other, *sofar)


def merge_kernel(left_ref, right_ref, out_ref, zero_ref):
    zero_ref[...] = jnp.zeros_like(zero_ref)
    gram = unit_trace(left_ref[...] + right_ref[...])
    keep = gram.shape[0] // 2
    first = lax.axis_index("tm") == 0
    swapped = pltpu.roll(pltpu.roll(gram, keep, 1), keep, 0)
    basis = basis_rows(jnp.where(first, gram, swapped), keep, zero_ref[...])
    half = out_ref.shape[0]
    out_ref[...] = jnp.where(first, basis[:half], pltpu.roll(basis[half:], keep, 1))


def merge_weights(left, right):
    order = left.shape[0]
    return pl.pallas_call(
        merge_kernel,
        out_shape=jax.ShapeDtypeStruct((order // 4, order), F32),
        in_specs=[pl.BlockSpec(memory_space=VMEM)] * 2,
        out_specs=pl.BlockSpec(memory_space=VMEM),
        scratch_shapes=[pltpu.VMEM((8, order), F32)],
        name="merge",
        compiler_params=grant(2),
    )(left, right)


def output_kernel(pieces, weights_ref, *refs):
    owns, others = refs[:pieces], refs[pieces : 2 * pieces]
    out_ref, held_ref, sems = refs[2 * pieces :]
    half = out_ref.shape[0]
    weights = jnp.concatenate(split(weights_ref[...]), axis=0)
    rows = owns[0].shape[1]
    copies = []
    for i in range(pieces):
        both = jnp.concatenate([owns[i][...], others[i][...]], axis=0)
        part = fast(weights, both)
        here = slice(i * rows, i * rows + rows)
        held_ref[:, here] = (part[:half] + part[half:]).astype(out_ref.dtype)
        copies.append(pltpu.make_async_copy(held_ref.at[:, here], out_ref.at[:, here], sems.at[i]))
        copies[-1].start()
    for copy in copies:
        copy.wait()


def output(weights, owns, others):
    keep = owns[0].shape[0]
    rows = sum(own.shape[1] for own in owns)
    shape = (keep // 2, rows)
    return pl.pallas_call(
        functools.partial(output_kernel, len(owns)),
        out_shape=jax.ShapeDtypeStruct(shape, jnp.bfloat16),
        in_specs=[pl.BlockSpec(memory_space=VMEM)] * (1 + 2 * len(owns)),
        out_specs=pl.BlockSpec(memory_space=pltpu.MemorySpace.HBM),
        scratch_shapes=[pltpu.VMEM(shape, jnp.bfloat16), pltpu.SemaphoreType.DMA((len(owns),))],
        name="output",
        compiler_params=grant(OUT_MB),
    )(weights, *owns, *others)


def flip(block, axis, mask):
    count = lax.axis_size(axis)
    return lax.ppermute(block, axis, [(i, i ^ mask) for i in range(count)])


def all_but_last_sum(value, axis):
    count = lax.axis_size(axis)
    masks = [1] + [(1 << bit + 1) - 2 for bit in range(1, count.bit_length() - 1)]
    for mask in masks[:-1]:
        value = value + flip(value, axis, mask)
    return value, flip(value, axis, masks[-1])


def block_of(rows, limit):
    size = min(rows, limit)
    while rows % size:
        size //= 2
    return size


def shards(prior, snapshots):
    keep = prior.shape[2]
    local, prior_t, frames = local_gram(prior[0].T, snapshots[0], block_of(prior.shape[1], CHUNK))
    rows = frames.shape[0]
    weights = steps_weights(*all_but_last_sum(local, "rows"), keep)
    piece = rows // PIECES
    owns, others = [], []
    for i in range(PIECES):
        owns.append(project(weights, prior_t, frames, i * piece, piece))
        others.append(flip(owns[-1], "tm", 1))
    gram = pair_gram(owns[0], others[0])
    for own, other in zip(owns[1:], others[1:]):
        gram = pair_gram(own, other, gram)
    final = merge_weights(*all_but_last_sum(gram, "rows"))
    return output(final, owns, others).T


def solution(mesh):
    in_specs = (P("tm", ("job", "rows"), None), P("tm", ("job", "rows"), None))
    out_specs = P(("job", "rows"), "tm")
    return jax.shard_map(shards, mesh=mesh, in_specs=in_specs, out_specs=out_specs, check_vma=False)
```

time: 129 us -> 97 us (0.75)
  Pallas kernels: 73 us -> 50.5 us
  waiting for transfers between devices: 41.8 us -> 26.3 us
  starting transfers between devices: 10.7 us -> 18.7 us
  local copies, waits for them, and re-layouts: 1.34 us -> 0 us
    ppermute x7 -> x10, waiting for transfers between devices: 41.8 us -> 26.3 us  [flip(): return lax.ppermute(block, axis, [(i, i ^ mask) for i in range(count)])]
    pallas_call x4 -> x10, Pallas kernels: 38.8 us -> 25.4 us  [the longest x1 15.1 us: local_gram(): pl.pallas_call(gram_kernel, out_shape=(jax.ShapeDtypeStruct((keep, 16 * k...]
    ppermute x7 -> x10, starting transfers between devices: 10.7 us -> 18.7 us  [flip(): return lax.ppermute(block, axis, [(i, i ^ mask) for i in range(count)])]
    pallas_call x1, Pallas kernels: 27.4 us -> 20.6 us  [steps_weights(): pl.pallas_call(steps_kernel, out_shape=jax.ShapeDtypeStruct((keep, width)...]
    pallas_call x1, Pallas kernels: 6.87 us -> 4.46 us  [merge_weights(): pl.pallas_call(merge_kernel, out_shape=jax.ShapeDtypeStruct((order // 4,...]
    unnamed x8 -> x0, local copies, waits for them, and re-layouts: 1.34 us -> none
  transfers between devices with their start and end apart: 7 -> 10, of which waited for: 7 -> 7; matrix products, arithmetic and copies ran while one was open for 0% -> 0% of each run, Pallas kernels for 0% -> 6%
where the time goes in v2:
time: 97 us; the launch traced here: 96.9 us
  Pallas kernels  50.5 us (52%)
  waiting for transfers between devices  26.3 us (27%)
  starting transfers between devices  18.7 us (19%)
  other arithmetic  1.03 us (1%)
    ppermute x10, waiting for transfers between devices, flip(): return lax.ppermute(block, axis, [(i, i ^ mask) for i in range(count)])  26.3 us
    pallas_call x1, Pallas kernels, steps_weights(): pl.pallas_call(steps_kernel, out_shape=jax.ShapeDtypeStruct((keep, width)...  20.6 us
    ppermute x10, starting transfers between devices, flip(): return lax.ppermute(block, axis, [(i, i ^ mask) for i in range(count)])  18.7 us
    pallas_call x1, Pallas kernels, local_gram(): pl.pallas_call(gram_kernel, out_shape=(jax.ShapeDtypeStruct((keep, 16 * k...  15.1 us
    pallas_call x4, Pallas kernels, project(): pl.pallas_call(functools.partial(modes_kernel, first), out_shape=OUTVM((k...  5.39 us
    pallas_call x1, Pallas kernels, merge_weights(): pl.pallas_call(merge_kernel, out_shape=jax.ShapeDtypeStruct((order // 4,...  4.46 us
    pallas_call x4, Pallas kernels, pair_gram(): pl.pallas_call(pair_kernel, out_shape=jax.ShapeDtypeStruct((2 * keep, 2 *...  2.83 us
    pallas_call x1, Pallas kernels, output(): pl.pallas_call(functools.partial(output_kernel, len(owns)), out_shape=jax...  2.16 us
  transfers between devices with their start and end apart: 10, of which 7 were waited for; matrix products, arithmetic and copies ran while one was open for 0% of the time, Pallas kernels for 6%

profile of v2, /device:TPU:0, one launch (start us, length us, event | category | flops | bytes accessed | tf_op | source)
XLA Modules:
  0.0 96.9 jit_solution(8159570242860805548)
XLA Ops:
  0.0 15.1 %gram.1 = (f32[64,1024]{1,0:T(8,128)}, bf16[64,32768]{1,0:T(8,128)(2,1)S(1)}, bf16[32768,256]{1,0:T(8,128)(2,1)S(1)}) custom-call(bf16[64,32768]{1,0:T(8,128)(2,1)} %bitcast.6, bf16[32768,256]{1,0:T(8,128)(2,1)} %bitcast.5), custom_call_target="tpu_custom_call" | custom-call | tf_op jit(solution)/shard_map/gram/pallas_call | solution.py:230
  15.1 3.1 %collective-permute-start = (f32[64,1024]{1,0:T(8,128)}, f32[64,1024]{1,0:T(8,128)S(1)}, u32[]{:S(2)}, u32[]{:S(2)}) collective-permute-start(f32[64,1024]{1,0:T(8,128)} %get-tuple-element.8), channel_id=1, source_target_pairs={{0,1},{1,0},{2,3},{3,2},{4,5},{5,4},{6,7},{7,6},{8,9},{9,8},{10,11... | collective-permute-start | bytes 786440 | tf_op jit(solution)/shard_map/ppermute | solution.py:357
  18.1 6.5 %collective-permute-done = f32[64,1024]{1,0:T(8,128)S(1)} collective-permute-done((f32[64,1024]{1,0:T(8,128)}, f32[64,1024]{1,0:T(8,128)S(1)}, u32[]{:S(2)}, u32[]{:S(2)}) %collective-permute-start) | collective-permute-done | bytes 262176 | tf_op jit(solution)/shard_map/ppermute | solution.py:357
  24.6 1.0 %add.12 = f32[64,1024]{1,0:T(8,128)S(1)} add(f32[64,1024]{1,0:T(8,128)} %get-tuple-element.8, f32[64,1024]{1,0:T(8,128)S(1)} %collective-permute-done) | non-fusion elementwise | flops 65536 | bytes 786432 | tf_op jit(solution)/shard_map/add | solution.py:364
  25.6 1.9 %collective-permute-start.1 = (f32[64,1024]{1,0:T(8,128)S(1)}, f32[64,1024]{1,0:T(8,128)S(1)}, u32[]{:S(2)}, u32[]{:S(2)}) collective-permute-start(f32[64,1024]{1,0:T(8,128)S(1)} %add.12), channel_id=1, source_target_pairs={{0,2},{1,3},{2,0},{3,1},{4,6},{5,7},{6,4},{7,5},{8,10},{9,11},{10,... | collective-permute-start | bytes 786440 | tf_op jit(solution)/shard_map/ppermute | solution.py:357
  27.5 5.7 %collective-permute-done.1 = f32[64,1024]{1,0:T(8,128)S(1)} collective-permute-done((f32[64,1024]{1,0:T(8,128)S(1)}, f32[64,1024]{1,0:T(8,128)S(1)}, u32[]{:S(2)}, u32[]{:S(2)}) %collective-permute-start.1) | collective-permute-done | bytes 262176 | tf_op jit(solution)/shard_map/ppermute | solution.py:357
  33.2 3.6 %collective-permute-start.2 = (f32[64,1024]{1,0:T(8,128)S(1)}, f32[64,1024]{1,0:T(8,128)S(1)}, u32[]{:S(2)}, u32[]{:S(2)}) collective-permute-start(f32[64,1024]{1,0:T(8,128)S(1)} %add.13.left_ref), channel_id=1, source_target_pairs={{0,6},{1,7},{2,4},{3,5},{4,2},{5,3},{6,0},{7,1},{8,14},{9,15},{10,... | collective-permute-start | bytes 786440 | tf_op jit(solution)/shard_map/ppermute | solution.py:357
  36.8 5.0 %collective-permute-done.2.right_ref = f32[64,1024]{1,0:T(8,128)S(1)} collective-permute-done((f32[64,1024]{1,0:T(8,128)S(1)}, f32[64,1024]{1,0:T(8,128)S(1)}, u32[]{:S(2)}, u32[]{:S(2)}) %collective-permute-start.2) | collective-permute-done | bytes 262176 | tf_op jit(solution)/shard_map/ppermute | solution.py:357
  41.8 20.6 %steps.1.weights_ref = f32[64,384]{1,0:T(8,128)S(1)} custom-call(f32[64,1024]{1,0:T(8,128)S(1)} %add.13.left_ref, f32[64,1024]{1,0:T(8,128)S(1)} %collective-permute-done.2.right_ref), custom_call_target="tpu_custom_call" | custom-call | tf_op jit(solution)/shard_map/steps/pallas_call | solution.py:174
  62.4 1.3 %project.7.own_ref.refs_0_ = bf16[64,8192]{1,0:T(8,128)(2,1)S(1)} custom-call(f32[64,384]{1,0:T(8,128)S(1)} %steps.1.weights_ref, bf16[64,32768]{1,0:T(8,128)(2,1)S(1)} %get-tuple-element.9.prior_ref, bf16[32768,256]{1,0:T(8,128)(2,1)S(1)} %get-tuple-element.10.frames_ref), custom_call_target="tpu_custom_call" | custom-call | tf_op jit(solution)/shard_map/project/pallas_call | solution.py:269
  63.7 0.1 collective-permute-start.6
  63.8 1.3 %project.6.own_ref.refs_1_ = bf16[64,8192]{1,0:T(8,128)(2,1)S(1)} custom-call(f32[64,384]{1,0:T(8,128)S(1)} %steps.1.weights_ref, bf16[64,32768]{1,0:T(8,128)(2,1)S(1)} %get-tuple-element.9.prior_ref, bf16[32768,256]{1,0:T(8,128)(2,1)S(1)} %get-tuple-element.10.frames_ref), custom_call_target="tpu_custom_call" | custom-call | tf_op jit(solution)/shard_map/project/pallas_call | solution.py:269
  65.2 0.6 collective-permute-start.5
  65.7 1.3 %project.5.own_ref.refs_2_ = bf16[64,8192]{1,0:T(8,128)(2,1)S(1)} custom-call(f32[64,384]{1,0:T(8,128)S(1)} %steps.1.weights_ref, bf16[64,32768]{1,0:T(8,128)(2,1)S(1)} %get-tuple-element.9.prior_ref, bf16[32768,256]{1,0:T(8,128)(2,1)S(1)} %get-tuple-element.10.frames_ref), custom_call_target="tpu_custom_call" | custom-call | tf_op jit(solution)/shard_map/project/pallas_call | solution.py:269
  67.1 0.1 collective-permute-start.4
  67.2 1.3 %project.4.own_ref.refs_3_ = bf16[64,8192]{1,0:T(8,128)(2,1)S(1)} custom-call(f32[64,384]{1,0:T(8,128)S(1)} %steps.1.weights_ref, bf16[64,32768]{1,0:T(8,128)(2,1)S(1)} %get-tuple-element.9.prior_ref, bf16[32768,256]{1,0:T(8,128)(2,1)S(1)} %get-tuple-element.10.frames_ref), custom_call_target="tpu_custom_call" | custom-call | tf_op jit(solution)/shard_map/project/pallas_call | solution.py:269
  68.5 0.6 collective-permute-start.3
  69.1 0.0 collective-permute-done.6.other_ref.refs_4_
  69.1 0.7 pair.4.rest_0_
  69.8 0.0 collective-permute-done.5.other_ref.refs_5_
  69.8 0.7 pair.5.rest_0_
  70.5 0.7 pair.6.rest_0_
  71.3 0.1 collective-permute-done.3.other_ref.refs_7_
  71.4 0.7 pair.7
  72.1 1.3 %collective-permute-start.7 = (f32[128,128]{1,0:T(8,128)S(1)}, f32[128,128]{1,0:T(8,128)S(1)}, u32[]{:S(2)}, u32[]{:S(2)}) collective-permute-start(f32[128,128]{1,0:T(8,128)S(1)} %pair.7), channel_id=1, source_target_pairs={{0,1},{1,0},{2,3},{3,2},{4,5},{5,4},{6,7},{7,6},{8,9},{9,8},{10,11... | collective-permute-start | bytes 196616 | tf_op jit(solution)/shard_map/ppermute | solution.py:357
  73.4 3.1 %collective-permute-done.7 = f32[128,128]{1,0:T(8,128)S(1)} collective-permute-done((f32[128,128]{1,0:T(8,128)S(1)}, f32[128,128]{1,0:T(8,128)S(1)}, u32[]{:S(2)}, u32[]{:S(2)}) %collective-permute-start.7) | collective-permute-done | bytes 65568 | tf_op jit(solution)/shard_map/ppermute | solution.py:357
  76.5 5.0 %collective-permute-start.8 = (f32[128,128]{1,0:T(8,128)S(1)}, f32[128,128]{1,0:T(8,128)S(1)}, u32[]{:S(2)}, u32[]{:S(2)}) collective-permute-start(f32[128,128]{1,0:T(8,128)S(1)} %add.14), channel_id=1, source_target_pairs={{0,2},{1,3},{2,0},{3,1},{4,6},{5,7},{6,4},{7,5},{8,10},{9,11},{10,... | collective-permute-start | bytes 196616 | tf_op jit(solution)/shard_map/ppermute | solution.py:357
  81.6 2.2 %collective-permute-done.8 = f32[128,128]{1,0:T(8,128)S(1)} collective-permute-done((f32[128,128]{1,0:T(8,128)S(1)}, f32[128,128]{1,0:T(8,128)S(1)}, u32[]{:S(2)}, u32[]{:S(2)}) %collective-permute-start.8) | collective-permute-done | bytes 65568 | tf_op jit(solution)/shard_map/ppermute | solution.py:357
  83.8 2.5 %collective-permute-start.9 = (f32[128,128]{1,0:T(8,128)S(1)}, f32[128,128]{1,0:T(8,128)S(1)}, u32[]{:S(2)}, u32[]{:S(2)}) collective-permute-start(f32[128,128]{1,0:T(8,128)S(1)} %add.15.left_ref), channel_id=1, source_target_pairs={{0,6},{1,7},{2,4},{3,5},{4,2},{5,3},{6,0},{7,1},{8,14},{9,15},{10,... | collective-permute-start | bytes 196616 | tf_op jit(solution)/shard_map/ppermute | solution.py:357
  86.4 3.7 %collective-permute-done.9.right_ref = f32[128,128]{1,0:T(8,128)S(1)} collective-permute-done((f32[128,128]{1,0:T(8,128)S(1)}, f32[128,128]{1,0:T(8,128)S(1)}, u32[]{:S(2)}, u32[]{:S(2)}) %collective-permute-start.9) | collective-permute-done | bytes 65568 | tf_op jit(solution)/shard_map/ppermute | solution.py:357
  90.1 4.5 %merge.1.weights_ref = f32[32,128]{1,0:T(8,128)S(1)} custom-call(f32[128,128]{1,0:T(8,128)S(1)} %add.15.left_ref, f32[128,128]{1,0:T(8,128)S(1)} %collective-permute-done.9.right_ref), custom_call_target="tpu_custom_call" | custom-call | tf_op jit(solution)/shard_map/merge/pallas_call | solution.py:311
  94.5 2.2 %output.1 = bf16[32,32768]{1,0:T(8,128)(2,1)} custom-call(f32[32,128]{1,0:T(8,128)S(1)} %merge.1.weights_ref, bf16[64,8192]{1,0:T(8,128)(2,1)S(1)} %project.7.own_ref.refs_0_, bf16[64,8192]{1,0:T(8,128)(2,1)S(1)} %project.6.own_ref.refs_1_, bf16[64,8192]{1,0:T(8,128)(2,1)S(1)} %project.5.own_ref.refs_2_, bf16[64,8192]{1,0:T(8,128)(2,1)S(1)} %project.4.own_ref.refs_3_, ...), custom_call_target="tpu_custom_call" | custom-call | tf_op jit(solution)/shard_map/output/pallas_call | solution.py:344
  (4 shorter events, 0.1 us)
Async XLA Ops:
  15.1 9.6 %collective-permute-start = (f32[64,1024]{1,0:T(8,128)}, f32[64,1024]{1,0:T(8,128)S(1)}, u32[]{:S(2)}, u32[]{:S(2)}) collective-permute-start(f32[64,1024]{1,0:T(8,128)} %get-tuple-element.8), channel_id=1, source_target_pairs={{0,1},{1,0},{2,3},{3,2},{4,5},{5,4},{6,7},{7,6},{8,9},{9,8},{10,11... | collective-permute-start | bytes 786440 | tf_op jit(solution)/shard_map/ppermute | solution.py:357
  25.6 7.5 %collective-permute-start.1 = (f32[64,1024]{1,0:T(8,128)S(1)}, f32[64,1024]{1,0:T(8,128)S(1)}, u32[]{:S(2)}, u32[]{:S(2)}) collective-permute-start(f32[64,1024]{1,0:T(8,128)S(1)} %add.12), channel_id=1, source_target_pairs={{0,2},{1,3},{2,0},{3,1},{4,6},{5,7},{6,4},{7,5},{8,10},{9,11},{10,... | collective-permute-start | bytes 786440 | tf_op jit(solution)/shard_map/ppermute | solution.py:357
  33.2 8.6 %collective-permute-start.2 = (f32[64,1024]{1,0:T(8,128)S(1)}, f32[64,1024]{1,0:T(8,128)S(1)}, u32[]{:S(2)}, u32[]{:S(2)}) collective-permute-start(f32[64,1024]{1,0:T(8,128)S(1)} %add.13.left_ref), channel_id=1, source_target_pairs={{0,6},{1,7},{2,4},{3,5},{4,2},{5,3},{6,0},{7,1},{8,14},{9,15},{10,... | collective-permute-start | bytes 786440 | tf_op jit(solution)/shard_map/ppermute | solution.py:357
  63.7 5.3 %collective-permute-start.6 = (bf16[64,8192]{1,0:T(8,128)(2,1)S(1)}, bf16[64,8192]{1,0:T(8,128)(2,1)S(1)}, u32[]{:S(2)}, u32[]{:S(2)}) collective-permute-start(bf16[64,8192]{1,0:T(8,128)(2,1)S(1)} %project.7.own_ref.refs_0_), channel_id=1, source_target_pairs={{0,8},{8,0},{1,9},{9,1},{2,10},{10,2},{3,11},{11,3},{4,12},{12,4},... | collective-permute-start | bytes 3145736 | tf_op jit(solution)/shard_map/ppermute | solution.py:357
  65.2 4.6 %collective-permute-start.5 = (bf16[64,8192]{1,0:T(8,128)(2,1)S(1)}, bf16[64,8192]{1,0:T(8,128)(2,1)S(1)}, u32[]{:S(2)}, u32[]{:S(2)}) collective-permute-start(bf16[64,8192]{1,0:T(8,128)(2,1)S(1)} %project.6.own_ref.refs_1_), channel_id=1, source_target_pairs={{0,8},{8,0},{1,9},{9,1},{2,10},{10,2},{3,11},{11,3},{4,12},{12,4},... | collective-permute-start | bytes 3145736 | tf_op jit(solution)/shard_map/ppermute | solution.py:357
  67.1 3.4 %collective-permute-start.4 = (bf16[64,8192]{1,0:T(8,128)(2,1)S(1)}, bf16[64,8192]{1,0:T(8,128)(2,1)S(1)}, u32[]{:S(2)}, u32[]{:S(2)}) collective-permute-start(bf16[64,8192]{1,0:T(8,128)(2,1)S(1)} %project.5.own_ref.refs_2_), channel_id=1, source_target_pairs={{0,8},{8,0},{1,9},{9,1},{2,10},{10,2},{3,11},{11,3},{4,12},{12,4},... | collective-permute-start | bytes 3145736 | tf_op jit(solution)/shard_map/ppermute | solution.py:357
  68.5 2.8 %collective-permute-start.3 = (bf16[64,8192]{1,0:T(8,128)(2,1)S(1)}, bf16[64,8192]{1,0:T(8,128)(2,1)S(1)}, u32[]{:S(2)}, u32[]{:S(2)}) collective-permute-start(bf16[64,8192]{1,0:T(8,128)(2,1)S(1)} %project.4.own_ref.refs_3_), channel_id=1, source_target_pairs={{0,8},{8,0},{1,9},{9,1},{2,10},{10,2},{3,11},{11,3},{4,12},{12,4},... | collective-permute-start | bytes 3145736 | tf_op jit(solution)/shard_map/ppermute | solution.py:357
  72.1 4.4 %collective-permute-start.7 = (f32[128,128]{1,0:T(8,128)S(1)}, f32[128,128]{1,0:T(8,128)S(1)}, u32[]{:S(2)}, u32[]{:S(2)}) collective-permute-start(f32[128,128]{1,0:T(8,128)S(1)} %pair.7), channel_id=1, source_target_pairs={{0,1},{1,0},{2,3},{3,2},{4,5},{5,4},{6,7},{7,6},{8,9},{9,8},{10,11... | collective-permute-start | bytes 196616 | tf_op jit(solution)/shard_map/ppermute | solution.py:357
  76.5 7.3 %collective-permute-start.8 = (f32[128,128]{1,0:T(8,128)S(1)}, f32[128,128]{1,0:T(8,128)S(1)}, u32[]{:S(2)}, u32[]{:S(2)}) collective-permute-start(f32[128,128]{1,0:T(8,128)S(1)} %add.14), channel_id=1, source_target_pairs={{0,2},{1,3},{2,0},{3,1},{4,6},{5,7},{6,4},{7,5},{8,10},{9,11},{10,... | collective-permute-start | bytes 196616 | tf_op jit(solution)/shard_map/ppermute | solution.py:357
  83.8 6.2 %collective-permute-start.9 = (f32[128,128]{1,0:T(8,128)S(1)}, f32[128,128]{1,0:T(8,128)S(1)}, u32[]{:S(2)}, u32[]{:S(2)}) collective-permute-start(f32[128,128]{1,0:T(8,128)S(1)} %add.15.left_ref), channel_id=1, source_target_pairs={{0,6},{1,7},{2,4},{3,5},{4,2},{5,3},{6,0},{7,1},{8,14},{9,15},{10,... | collective-permute-start | bytes 196616 | tf_op jit(solution)/shard_map/ppermute | solution.py:357

commit v3 on v2

--- a/solution.py
+++ b/solution.py
@@ -15,9 +15,8 @@
 TN = (((0,), (0,)), ((), ()))
 VMEM = pltpu.MemorySpace.VMEM
 PIECES = 4
-CHUNK = 4096
+AHEAD = 2
 GRAM_MB, PROJ_MB, PAIR_MB, OUT_MB = 36, 12, 6, 8
-OUTVM = pltpu.VMEM
 
 
 def dot(a, b, dims=NN):
@@ -118,38 +117,49 @@
 
 def unpack(packed, keep):
     tile = lambda i: packed[:, 128 * i : 128 * i + 128]
-    lane = iota((keep, 128), 1)
+    lane, row = iota((keep, 128), 1), iota((keep, 128), 0)
     zero = jnp.zeros((keep, 128), F32)
+    mixed = tile(6)
+    diag = jnp.where(
+        lane == 127,
+        pltpu.roll(jnp.broadcast_to(mixed[keep - 2 : keep - 1], mixed.shape), 127, 1),
+        pltpu.roll(jnp.broadcast_to(mixed[keep - 1 : keep], mixed.shape), keep, 1),
+    )
+    end = jnp.where(lane == row + keep, diag, pltpu.roll(tile(0), keep, 1))
     upper = jnp.concatenate(
         [
             jnp.concatenate([tile(0), tile(1)], axis=1),
-            jnp.concatenate([tile(6), tile(2)], axis=1),
+            jnp.concatenate([mixed, tile(2)], axis=1),
             jnp.concatenate([zero, tile(3)], axis=1),
-            jnp.concatenate([zero, tile(7)], axis=1),
+            jnp.concatenate([zero, end], axis=1),
         ],
         axis=0,
     )
     size = upper.shape[0]
-    row_block = iota((size, size), 0) // keep
-    col_block = iota((size, size), 1) // keep
-    square = jnp.where(row_block <= col_block, upper, upper.T)
+    high, wide = iota((size, size), 0), iota((size, size), 1)
+    last = size - keep
+    held = ((high <= wide) & (wide < last)) | ((high < last) & (wide >= last))
+    held |= (high >= wide) & (high >= last) & (wide >= last)
+    square = jnp.where(held, upper, upper.T)
     cross = jnp.concatenate([tile(4), tile(5)], axis=1)
-    corner = jnp.where(lane < keep, tile(6), 0.0)
+    turned = jnp.concatenate([mixed, mixed], axis=0).T[:keep]
+    corner = jnp.where(lane < keep, jnp.where(row <= lane, mixed, turned), 0.0)
     low = jnp.concatenate([cross, corner], axis=1)
     cross_pad = jnp.concatenate([cross, jnp.zeros_like(cross)], axis=0)
     top = jnp.concatenate([square, cross_pad.T], axis=1)
     return jnp.concatenate([top, low, jnp.zeros_like(low)], axis=0)
 
 
-def unit_trace(gram):
-    eye = iota(gram.shape, 0) == iota(gram.shape, 1)
-    return gram / jnp.sum(jnp.where(eye, gram, 0.0))
-
-
-def steps_kernel(left_ref, right_ref, out_ref, total_ref, both_ref, zero_ref):
+def trace(gram):
+    return jnp.sum(jnp.where(iota(gram.shape, 0) == iota(gram.shape, 1), gram, 0.0))
+
+
+def steps_kernel(left_ref, right_ref, out_ref, modes_ref, total_ref, both_ref, zero_ref):
     keep = left_ref.shape[0]
     zero_ref[...] = jnp.zeros_like(zero_ref)
-    total = unit_trace(unpack(left_ref[...] + right_ref[...], keep))
+    total = unpack(left_ref[...] + right_ref[...], keep)
+    scale = trace(total)
+    total = total * (1.0 / scale)
     total_ref[...] = total
     width = total.shape[0]
     frames = STEPS * keep
@@ -167,15 +177,19 @@
         both_ref[:keep] = dot(basis_rows(gram, keep, zero_ref[...]), both)
 
     out_ref[...] = both_ref[:keep, width:]
+    modes_ref[...] = dot(both_ref[:keep, :width], both_ref[:keep, width:], NT) * scale
 
 
 def steps_weights(left, right, keep):
     width = (STEPS + 2) * keep
     return pl.pallas_call(
         steps_kernel,
-        out_shape=jax.ShapeDtypeStruct((keep, width), F32),
+        out_shape=(
+            jax.ShapeDtypeStruct((keep, width), F32),
+            jax.ShapeDtypeStruct((keep, keep), F32),
+        ),
         in_specs=[pl.BlockSpec(memory_space=VMEM)] * 2,
-        out_specs=pl.BlockSpec(memory_space=VMEM),
+        out_specs=[pl.BlockSpec(memory_space=VMEM)] * 2,
         scratch_shapes=[
             pltpu.VMEM((width, width), F32),
             pltpu.VMEM((2 * keep, 2 * width), F32),
@@ -186,58 +200,65 @@
     )(left, right)
 
 
-def gram_kernel(prior_in, frames_in, out_ref, prior_ref, frames_ref, sems, square_ref, corner_ref):
-    keep, rows = prior_ref.shape
-    width = frames_ref.shape[1]
-    count = sems.shape[1]
-    size = rows // count
+def gram_kernel(cuts, prior_in, frames_in, out_ref, prior_ref, frames_ref, sems, square_ref, corner_ref):
+    keep = prior_ref.shape[0]
+    blocks = [slice(low, high) for low, high in zip(cuts[:-1], cuts[1:])]
 
     def copies(i):
-        at = slice(i * size, i * size + size)
+        at = blocks[i]
         return (
             pltpu.make_async_copy(prior_in.at[:, at], prior_ref.at[:, at], sems.at[0, i]),
             pltpu.make_async_copy(frames_in.at[at], frames_ref.at[at], sems.at[1, i]),
         )
 
-    for i in range(count):
+    for i in range(min(AHEAD, len(blocks))):
         for copy in copies(i):
             copy.start()
-    for i in range(count):
+    for i, at in enumerate(blocks):
         for copy in copies(i):
             copy.wait()
-        at = slice(i * size, i * size + size)
+        if i + AHEAD < len(blocks):
+            for copy in copies(i + AHEAD):
+                copy.start()
         frames = frames_ref[at]
         prior = prior_ref[:, at]
-        part = fast(jnp.concatenate([frames.T, prior], axis=0), frames)
+        part = jnp.concatenate([fast(frames, frames, TN), fast(prior, frames)], axis=0)
         last = fast(prior, prior, NT)
         square_ref[...] = part if i == 0 else square_ref[...] + part
         corner_ref[...] = last if i == 0 else corner_ref[...] + last
 
     corner = corner_ref[...]
     wide = jnp.concatenate([corner, jnp.zeros_like(corner)], axis=1)
-    lane = iota(wide.shape, 1)
-    out_ref[:, 0:256] = square_ref[0:64]
+    lane, row = iota(wide.shape, 1), iota(wide.shape, 0)
+    end = square_ref[192:256, 128:256]
+    diag = jnp.sum(jnp.where(lane == row + keep, end, 0.0), axis=0, keepdims=True)
+    diag = jnp.broadcast_to(diag, end.shape)
+    mixed = jnp.where(lane < keep, wide, square_ref[64:128, 0:128])
+    mixed = jnp.where((row == keep - 1) & (lane < keep - 1), pltpu.roll(diag, keep, 1), mixed)
+    mixed = jnp.where((row == keep - 2) & (lane == 0), pltpu.roll(diag, 1, 1), mixed)
+    free = (lane < keep) & (row > lane)
+    out_ref[:, 0:128] = jnp.where(free, pltpu.roll(end, keep, 1), square_ref[0:64, 0:128])
+    out_ref[:, 128:256] = square_ref[0:64, 128:256]
     out_ref[:, 256:384] = square_ref[64:128, 128:256]
     out_ref[:, 384:512] = square_ref[128:192, 128:256]
     out_ref[:, 512:768] = square_ref[256:320]
-    out_ref[:, 768:896] = jnp.where(lane < keep, wide, square_ref[64:128, 0:128])
-    out_ref[:, 896:1024] = square_ref[192:256, 128:256]
-
-
-def local_gram(prior_t, frames, size):
+    out_ref[:, 768:896] = mixed
+
+
+def local_gram(prior_t, frames, cuts):
     keep, rows = prior_t.shape
     width = frames.shape[1]
     return pl.pallas_call(
-        gram_kernel,
+        functools.partial(gram_kernel, cuts),
         out_shape=(
-            jax.ShapeDtypeStruct((keep, 16 * keep), F32),
-            OUTVM(prior_t.shape, prior_t.dtype),
-            OUTVM(frames.shape, frames.dtype),
+            jax.ShapeDtypeStruct((keep, 14 * keep), F32),
+            pltpu.VMEM(prior_t.shape, prior_t.dtype),
+            pltpu.VMEM(frames.shape, frames.dtype),
         ),
         in_specs=[pl.BlockSpec(memory_space=pltpu.MemorySpace.HBM)] * 2,
         out_specs=[pl.BlockSpec(memory_space=VMEM)] * 3,
         scratch_shapes=[
-            pltpu.SemaphoreType.DMA((2, rows // size)),
+            pltpu.SemaphoreType.DMA((2, len(cuts) - 1)),
             pltpu.VMEM((width + keep, width), F32),
             pltpu.VMEM((keep, keep), F32),
         ],
@@ -268,7 +289,7 @@
     keep = prior_t.shape[0]
     return pl.pallas_call(
         functools.partial(modes_kernel, first),
-        out_shape=OUTVM((keep, rows), jnp.bfloat16),
+        out_shape=pltpu.VMEM((keep, rows), jnp.bfloat16),
         in_specs=[pl.BlockSpec(memory_space=VMEM)] * 3,
         out_specs=pl.BlockSpec(memory_space=VMEM),
         name="project",
@@ -278,8 +299,9 @@
 
 def pair_kernel(own_ref, other_ref, *rest):
     out_ref = rest[-1]
-    both = jnp.concatenate([own_ref[...], other_ref[...]], axis=0)
-    gram = fast(both, both, NT)
+    half = out_ref.shape[0]
+    gram = fast(own_ref[...], other_ref[...], NT)
+    gram = jnp.concatenate([gram[:half], gram[half:]], axis=1)
     out_ref[...] = rest[0][...] + gram if len(rest) > 1 else gram
 
 
@@ -287,7 +309,7 @@
     keep = own.shape[0]
     return pl.pallas_call(
         pair_kernel,
-        out_shape=jax.ShapeDtypeStruct((2 * keep, 2 * keep), F32),
+        out_shape=jax.ShapeDtypeStruct((keep // 2, 2 * keep), F32),
         in_specs=[pl.BlockSpec(memory_space=VMEM)] * (2 + len(sofar)),
         out_specs=pl.BlockSpec(memory_space=VMEM),
         name="pair",
@@ -295,10 +317,19 @@
     )(own, other, *sofar)
 
 
-def merge_kernel(left_ref, right_ref, out_ref, zero_ref):
+def merge_kernel(left_ref, right_ref, own_ref, other_ref, out_ref, zero_ref):
     zero_ref[...] = jnp.zeros_like(zero_ref)
-    gram = unit_trace(left_ref[...] + right_ref[...])
-    keep = gram.shape[0] // 2
+    keep = own_ref.shape[0]
+    halves = left_ref[...] + right_ref[...]
+    cross = jnp.concatenate([halves[:, :keep], halves[:, keep:]], axis=0)
+    gram = jnp.concatenate(
+        [
+            jnp.concatenate([own_ref[...], cross], axis=1),
+            jnp.concatenate([cross.T, other_ref[...]], axis=1),
+        ],
+        axis=0,
+    )
+    gram = gram * (1.0 / trace(gram))
     first = lax.axis_index("tm") == 0
     swapped = pltpu.roll(pltpu.roll(gram, keep, 1), keep, 0)
     basis = basis_rows(jnp.where(first, gram, swapped), keep, zero_ref[...])
@@ -306,17 +337,17 @@
     out_ref[...] = jnp.where(first, basis[:half], pltpu.roll(basis[half:], keep, 1))
 
 
-def merge_weights(left, right):
-    order = left.shape[0]
+def merge_weights(left, right, own, other):
+    keep = own.shape[0]
     return pl.pallas_call(
         merge_kernel,
-        out_shape=jax.ShapeDtypeStruct((order // 4, order), F32),
-        in_specs=[pl.BlockSpec(memory_space=VMEM)] * 2,
+        out_shape=jax.ShapeDtypeStruct((keep // 2, 2 * keep), F32),
+        in_specs=[pl.BlockSpec(memory_space=VMEM)] * 4,
         out_specs=pl.BlockSpec(memory_space=VMEM),
-        scratch_shapes=[pltpu.VMEM((8, order), F32)],
+        scratch_shapes=[pltpu.VMEM((8, 2 * keep), F32)],
         name="merge",
         compiler_params=grant(2),
-    )(left, right)
+    )(left, right, own, other)
 
 
 def output_kernel(pieces, weights_ref, *refs):
@@ -357,12 +388,19 @@
     return lax.ppermute(block, axis, [(i, i ^ mask) for i in range(count)])
 
 
-def all_but_last_sum(value, axis):
+def all_but_last_sum(value, axis, mirror):
     count = lax.axis_size(axis)
-    masks = [1] + [(1 << bit + 1) - 2 for bit in range(1, count.bit_length() - 1)]
+    masks = [1 << bit for bit in range(count.bit_length() - 1)]
+    if mirror:
+        masks = masks[:1] + [2 * mask - 2 for mask in masks[1:]]
     for mask in masks[:-1]:
         value = value + flip(value, axis, mask)
     return value, flip(value, axis, masks[-1])
+
+
+def cuts_of(rows):
+    unit = rows // 32
+    return [unit * at for at in (0, 1, 4, 12, 20, 28, 32)]
 
 
 def block_of(rows, limit):
@@ -374,18 +412,19 @@
 
 def shards(prior, snapshots):
     keep = prior.shape[2]
-    local, prior_t, frames = local_gram(prior[0].T, snapshots[0], block_of(prior.shape[1], CHUNK))
-    rows = frames.shape[0]
-    weights = steps_weights(*all_but_last_sum(local, "rows"), keep)
+    rows = prior.shape[1]
+    local, prior_t, frames = local_gram(prior[0].T, snapshots[0], cuts_of(rows))
+    weights, own_gram = steps_weights(*all_but_last_sum(local, "rows", True), keep)
+    other_gram = flip(own_gram, "tm", 1)
     piece = rows // PIECES
     owns, others = [], []
     for i in range(PIECES):
         owns.append(project(weights, prior_t, frames, i * piece, piece))
         others.append(flip(owns[-1], "tm", 1))
-    gram = pair_gram(owns[0], others[0])
+    cross = pair_gram(owns[0], others[0])
     for own, other in zip(owns[1:], others[1:]):
-        gram = pair_gram(own, other, gram)
-    final = merge_weights(*all_but_last_sum(gram, "rows"))
+        cross = pair_gram(own, other, cross)
+    final = merge_weights(*all_but_last_sum(cross, "rows", False), own_gram, other_gram)
     return output(final, owns, others).T
 
 

time: 97 us -> 89.8 us (0.926)
  waiting for transfers between devices: 26.3 us -> 21.6 us
  Pallas kernels: 50.5 us -> 48.3 us
    ppermute x10 -> x11, waiting for transfers between devices: 26.3 us -> 21.6 us  [flip(): return lax.ppermute(block, axis, [(i, i ^ mask) for i in range(count)])]
    pallas_call x11, Pallas kernels: 48.3 us -> 46.1 us  [the longest x1 20.9 us: steps_weights(): pl.pallas_call(steps_kernel, out_shape=(jax.ShapeDtypeStruct((keep, width...]
    ppermute x10 -> x11, starting transfers between devices: 18.7 us -> 18.5 us  [flip(): return lax.ppermute(block, axis, [(i, i ^ mask) for i in range(count)])]
  transfers between devices with their start and end apart: 10 -> 11, of which waited for: 7 -> 7; matrix products, arithmetic and copies ran while one was open for 0% -> 0% of each run, Pallas kernels for 6% -> 6%
where the time goes in v3:
time: 89.8 us; the launch traced here: 89.7 us
  Pallas kernels  48.3 us (54%)
  waiting for transfers between devices  21.6 us (24%)
  starting transfers between devices  18.5 us (21%)
  other arithmetic  1 us (1%)
    ppermute x11, waiting for transfers between devices, flip(): return lax.ppermute(block, axis, [(i, i ^ mask) for i in range(count)])  21.6 us
    pallas_call x1, Pallas kernels, steps_weights(): pl.pallas_call(steps_kernel, out_shape=(jax.ShapeDtypeStruct((keep, width...  20.9 us
    ppermute x11, starting transfers between devices, flip(): return lax.ppermute(block, axis, [(i, i ^ mask) for i in range(count)])  18.5 us
    pallas_call x1, Pallas kernels, local_gram(): pl.pallas_call(functools.partial(gram_kernel, cuts), out_shape=(jax.Shape...  13.2 us
    pallas_call x4, Pallas kernels, project(): pl.pallas_call(functools.partial(modes_kernel, first), out_shape=pltpu.VM...  5.39 us
    pallas_call x1, Pallas kernels, merge_weights(): pl.pallas_call(merge_kernel, out_shape=jax.ShapeDtypeStruct((keep // 2, 2...  4.66 us
    pallas_call x1, Pallas kernels, output(): pl.pallas_call(functools.partial(output_kernel, len(owns)), out_shape=jax...  2.16 us
    pallas_call x4, Pallas kernels, pair_gram(): pl.pallas_call(pair_kernel, out_shape=jax.ShapeDtypeStruct((keep // 2, 2...  1.93 us
  transfers between devices with their start and end apart: 11, of which 7 were waited for; matrix products, arithmetic and copies ran while one was open for 0% of the time, Pallas kernels for 6%

profile of v3, /device:TPU:0, one launch (start us, length us, event | category | flops | bytes accessed | tf_op | source)
XLA Modules:
  0.0 89.7 jit_solution(2095831910465308332)
XLA Ops:
  0.0 13.2 %gram.1 = (f32[64,896]{1,0:T(8,128)}, bf16[64,32768]{1,0:T(8,128)(2,1)S(1)}, bf16[32768,256]{1,0:T(8,128)(2,1)S(1)}) custom-call(bf16[64,32768]{1,0:T(8,128)(2,1)} %bitcast.6, bf16[32768,256]{1,0:T(8,128)(2,1)} %bitcast.5), custom_call_target="tpu_custom_call" | custom-call | tf_op jit(solution)/shard_map/gram/pallas_call | solution.py:251
  13.2 3.1 %collective-permute-start = (f32[64,896]{1,0:T(8,128)}, f32[64,896]{1,0:T(8,128)S(1)}, u32[]{:S(2)}, u32[]{:S(2)}) collective-permute-start(f32[64,896]{1,0:T(8,128)} %get-tuple-element.10), channel_id=1, source_target_pairs={{0,1},{1,0},{2,3},{3,2},{4,5},{5,4},{6,7},{7,6},{8,9},{9,8},{10,11... | collective-permute-start | bytes 688136 | tf_op jit(solution)/shard_map/ppermute | solution.py:388
  16.3 5.8 %collective-permute-done = f32[64,896]{1,0:T(8,128)S(1)} collective-permute-done((f32[64,896]{1,0:T(8,128)}, f32[64,896]{1,0:T(8,128)S(1)}, u32[]{:S(2)}, u32[]{:S(2)}) %collective-permute-start) | collective-permute-done | bytes 229408 | tf_op jit(solution)/shard_map/ppermute | solution.py:388
  22.1 1.0 %add.12 = f32[64,896]{1,0:T(8,128)S(1)} add(f32[64,896]{1,0:T(8,128)} %get-tuple-element.10, f32[64,896]{1,0:T(8,128)S(1)} %collective-permute-done) | non-fusion elementwise | flops 57344 | bytes 688128 | tf_op jit(solution)/shard_map/add | solution.py:397
  23.1 1.9 %collective-permute-start.1 = (f32[64,896]{1,0:T(8,128)S(1)}, f32[64,896]{1,0:T(8,128)S(1)}, u32[]{:S(2)}, u32[]{:S(2)}) collective-permute-start(f32[64,896]{1,0:T(8,128)S(1)} %add.12), channel_id=1, source_target_pairs={{0,2},{1,3},{2,0},{3,1},{4,6},{5,7},{6,4},{7,5},{8,10},{9,11},{10,... | collective-permute-start | bytes 688136 | tf_op jit(solution)/shard_map/ppermute | solution.py:388
  24.9 5.0 %collective-permute-done.1 = f32[64,896]{1,0:T(8,128)S(1)} collective-permute-done((f32[64,896]{1,0:T(8,128)S(1)}, f32[64,896]{1,0:T(8,128)S(1)}, u32[]{:S(2)}, u32[]{:S(2)}) %collective-permute-start.1) | collective-permute-done | bytes 229408 | tf_op jit(solution)/shard_map/ppermute | solution.py:388
  29.9 3.6 %collective-permute-start.2 = (f32[64,896]{1,0:T(8,128)S(1)}, f32[64,896]{1,0:T(8,128)S(1)}, u32[]{:S(2)}, u32[]{:S(2)}) collective-permute-start(f32[64,896]{1,0:T(8,128)S(1)} %add.13.left_ref), channel_id=1, source_target_pairs={{0,6},{1,7},{2,4},{3,5},{4,2},{5,3},{6,0},{7,1},{8,14},{9,15},{10,... | collective-permute-start | bytes 688136 | tf_op jit(solution)/shard_map/ppermute | solution.py:388
  33.6 4.3 %collective-permute-done.2.right_ref = f32[64,896]{1,0:T(8,128)S(1)} collective-permute-done((f32[64,896]{1,0:T(8,128)S(1)}, f32[64,896]{1,0:T(8,128)S(1)}, u32[]{:S(2)}, u32[]{:S(2)}) %collective-permute-start.2) | collective-permute-done | bytes 229408 | tf_op jit(solution)/shard_map/ppermute | solution.py:388
  37.8 20.9 %steps.1 = (f32[64,384]{1,0:T(8,128)S(1)}, f32[64,64]{1,0:T(8,128)S(1)}) custom-call(f32[64,896]{1,0:T(8,128)S(1)} %add.13.left_ref, f32[64,896]{1,0:T(8,128)S(1)} %collective-permute-done.2.right_ref), custom_call_target="tpu_custom_call" | custom-call | tf_op jit(solution)/shard_map/steps/pallas_call | solution.py:185
  58.8 1.3 %project.7.own_ref.refs_0_ = bf16[64,8192]{1,0:T(8,128)(2,1)S(1)} custom-call(f32[64,384]{1,0:T(8,128)S(1)} %get-tuple-element.11.weights_ref, bf16[64,32768]{1,0:T(8,128)(2,1)S(1)} %get-tuple-element.12.prior_ref, bf16[32768,256]{1,0:T(8,128)(2,1)S(1)} %get-tuple-element.13.frames_ref), custom_call_target="tpu_custom_call" | custom-call | tf_op jit(solution)/shard_map/project/pallas_call | solution.py:290
  60.1 0.1 collective-permute-start.6
  60.2 1.3 %project.6.own_ref.refs_1_ = bf16[64,8192]{1,0:T(8,128)(2,1)S(1)} custom-call(f32[64,384]{1,0:T(8,128)S(1)} %get-tuple-element.11.weights_ref, bf16[64,32768]{1,0:T(8,128)(2,1)S(1)} %get-tuple-element.12.prior_ref, bf16[32768,256]{1,0:T(8,128)(2,1)S(1)} %get-tuple-element.13.frames_ref), custom_call_target="tpu_custom_call" | custom-call | tf_op jit(solution)/shard_map/project/pallas_call | solution.py:290
  61.6 0.6 collective-permute-start.5
  62.1 1.3 %project.5.own_ref.refs_2_ = bf16[64,8192]{1,0:T(8,128)(2,1)S(1)} custom-call(f32[64,384]{1,0:T(8,128)S(1)} %get-tuple-element.11.weights_ref, bf16[64,32768]{1,0:T(8,128)(2,1)S(1)} %get-tuple-element.12.prior_ref, bf16[32768,256]{1,0:T(8,128)(2,1)S(1)} %get-tuple-element.13.frames_ref), custom_call_target="tpu_custom_call" | custom-call | tf_op jit(solution)/shard_map/project/pallas_call | solution.py:290
  63.5 0.1 collective-permute-start.4
  63.5 1.3 %project.4.own_ref.refs_3_ = bf16[64,8192]{1,0:T(8,128)(2,1)S(1)} custom-call(f32[64,384]{1,0:T(8,128)S(1)} %get-tuple-element.11.weights_ref, bf16[64,32768]{1,0:T(8,128)(2,1)S(1)} %get-tuple-element.12.prior_ref, bf16[32768,256]{1,0:T(8,128)(2,1)S(1)} %get-tuple-element.13.frames_ref), custom_call_target="tpu_custom_call" | custom-call | tf_op jit(solution)/shard_map/project/pallas_call | solution.py:290
  64.9 0.6 collective-permute-start.3
  65.5 0.0 collective-permute-done.6.other_ref.refs_4_
  65.5 0.5 pair.4.rest_0_
  66.0 0.5 pair.5.rest_0_
  66.4 0.0 collective-permute-done.4.other_ref.refs_6_
  66.5 0.5 pair.6.rest_0_
  66.9 0.8 collective-permute-done.3.other_ref.refs_7_
  67.8 0.5 pair.7
  68.2 1.5 %collective-permute-start.7 = (f32[32,128]{1,0:T(8,128)S(1)}, f32[32,128]{1,0:T(8,128)S(1)}, u32[]{:S(2)}, u32[]{:S(2)}) collective-permute-start(f32[32,128]{1,0:T(8,128)S(1)} %pair.7), channel_id=1, source_target_pairs={{0,1},{1,0},{2,3},{3,2},{4,5},{5,4},{6,7},{7,6},{8,9},{9,8},{10,11... | collective-permute-start | bytes 49160 | tf_op jit(solution)/shard_map/ppermute | solution.py:388
  69.7 2.3 %collective-permute-done.7 = f32[32,128]{1,0:T(8,128)S(1)} collective-permute-done((f32[32,128]{1,0:T(8,128)S(1)}, f32[32,128]{1,0:T(8,128)S(1)}, u32[]{:S(2)}, u32[]{:S(2)}) %collective-permute-start.7) | collective-permute-done | bytes 16416 | tf_op jit(solution)/shard_map/ppermute | solution.py:388
  72.0 4.2 %collective-permute-start.8 = (f32[32,128]{1,0:T(8,128)S(1)}, f32[32,128]{1,0:T(8,128)S(1)}, u32[]{:S(2)}, u32[]{:S(2)}) collective-permute-start(f32[32,128]{1,0:T(8,128)S(1)} %add.14), channel_id=1, source_target_pairs={{0,2},{1,3},{2,0},{3,1},{4,6},{5,7},{6,4},{7,5},{8,10},{9,11},{10,... | collective-permute-start | bytes 49160 | tf_op jit(solution)/shard_map/ppermute | solution.py:388
  76.2 1.7 %collective-permute-done.8 = f32[32,128]{1,0:T(8,128)S(1)} collective-permute-done((f32[32,128]{1,0:T(8,128)S(1)}, f32[32,128]{1,0:T(8,128)S(1)}, u32[]{:S(2)}, u32[]{:S(2)}) %collective-permute-start.8) | collective-permute-done | bytes 16416 | tf_op jit(solution)/shard_map/ppermute | solution.py:388
  78.0 3.0 %collective-permute-start.9 = (f32[32,128]{1,0:T(8,128)S(1)}, f32[32,128]{1,0:T(8,128)S(1)}, u32[]{:S(2)}, u32[]{:S(2)}) collective-permute-start(f32[32,128]{1,0:T(8,128)S(1)} %add.15.left_ref), channel_id=1, source_target_pairs={{0,4},{1,5},{2,6},{3,7},{4,0},{5,1},{6,2},{7,3},{8,12},{9,13},{10,... | collective-permute-start | bytes 49160 | tf_op jit(solution)/shard_map/ppermute | solution.py:388
  81.0 1.7 %collective-permute-done.9.right_ref = f32[32,128]{1,0:T(8,128)S(1)} collective-permute-done((f32[32,128]{1,0:T(8,128)S(1)}, f32[32,128]{1,0:T(8,128)S(1)}, u32[]{:S(2)}, u32[]{:S(2)}) %collective-permute-start.9) | collective-permute-done | bytes 16416 | tf_op jit(solution)/shard_map/ppermute | solution.py:388
  82.7 4.7 %merge.1.weights_ref = f32[32,128]{1,0:T(8,128)S(1)} custom-call(f32[32,128]{1,0:T(8,128)S(1)} %add.15.left_ref, f32[32,128]{1,0:T(8,128)S(1)} %collective-permute-done.9.right_ref, f32[64,64]{1,0:T(8,128)S(1)} %get-tuple-element.14.own_ref, f32[64,64]{1,0:T(8,128)S(1)} %collective-permute-done.10.other_ref), custom_call_target="tpu_custom_call" | custom-call | tf_op jit(solution)/shard_map/merge/pallas_call | solution.py:342
  87.3 2.2 %output.1 = bf16[32,32768]{1,0:T(8,128)(2,1)} custom-call(f32[32,128]{1,0:T(8,128)S(1)} %merge.1.weights_ref, bf16[64,8192]{1,0:T(8,128)(2,1)S(1)} %project.7.own_ref.refs_0_, bf16[64,8192]{1,0:T(8,128)(2,1)S(1)} %project.6.own_ref.refs_1_, bf16[64,8192]{1,0:T(8,128)(2,1)S(1)} %project.5.own_ref.refs_2_, bf16[64,8192]{1,0:T(8,128)(2,1)S(1)} %project.4.own_ref.refs_3_, ...), custom_call_target="tpu_custom_call" | custom-call | tf_op jit(solution)/shard_map/output/pallas_call | solution.py:375
  (6 shorter events, 0.0 us)
Async XLA Ops:
  13.2 8.9 %collective-permute-start = (f32[64,896]{1,0:T(8,128)}, f32[64,896]{1,0:T(8,128)S(1)}, u32[]{:S(2)}, u32[]{:S(2)}) collective-permute-start(f32[64,896]{1,0:T(8,128)} %get-tuple-element.10), channel_id=1, source_target_pairs={{0,1},{1,0},{2,3},{3,2},{4,5},{5,4},{6,7},{7,6},{8,9},{9,8},{10,11... | collective-permute-start | bytes 688136 | tf_op jit(solution)/shard_map/ppermute | solution.py:388
  23.1 6.8 %collective-permute-start.1 = (f32[64,896]{1,0:T(8,128)S(1)}, f32[64,896]{1,0:T(8,128)S(1)}, u32[]{:S(2)}, u32[]{:S(2)}) collective-permute-start(f32[64,896]{1,0:T(8,128)S(1)} %add.12), channel_id=1, source_target_pairs={{0,2},{1,3},{2,0},{3,1},{4,6},{5,7},{6,4},{7,5},{8,10},{9,11},{10,... | collective-permute-start | bytes 688136 | tf_op jit(solution)/shard_map/ppermute | solution.py:388
  29.9 7.9 %collective-permute-start.2 = (f32[64,896]{1,0:T(8,128)S(1)}, f32[64,896]{1,0:T(8,128)S(1)}, u32[]{:S(2)}, u32[]{:S(2)}) collective-permute-start(f32[64,896]{1,0:T(8,128)S(1)} %add.13.left_ref), channel_id=1, source_target_pairs={{0,6},{1,7},{2,4},{3,5},{4,2},{5,3},{6,0},{7,1},{8,14},{9,15},{10,... | collective-permute-start | bytes 688136 | tf_op jit(solution)/shard_map/ppermute | solution.py:388
  60.1 5.3 %collective-permute-start.6 = (bf16[64,8192]{1,0:T(8,128)(2,1)S(1)}, bf16[64,8192]{1,0:T(8,128)(2,1)S(1)}, u32[]{:S(2)}, u32[]{:S(2)}) collective-permute-start(bf16[64,8192]{1,0:T(8,128)(2,1)S(1)} %project.7.own_ref.refs_0_), channel_id=1, source_target_pairs={{0,8},{8,0},{1,9},{9,1},{2,10},{10,2},{3,11},{11,3},{4,12},{12,4},... | collective-permute-start | bytes 3145736 | tf_op jit(solution)/shard_map/ppermute | solution.py:388
  61.6 4.4 %collective-permute-start.5 = (bf16[64,8192]{1,0:T(8,128)(2,1)S(1)}, bf16[64,8192]{1,0:T(8,128)(2,1)S(1)}, u32[]{:S(2)}, u32[]{:S(2)}) collective-permute-start(bf16[64,8192]{1,0:T(8,128)(2,1)S(1)} %project.6.own_ref.refs_1_), channel_id=1, source_target_pairs={{0,8},{8,0},{1,9},{9,1},{2,10},{10,2},{3,11},{11,3},{4,12},{12,4},... | collective-permute-start | bytes 3145736 | tf_op jit(solution)/shard_map/ppermute | solution.py:388
  63.5 3.0 %collective-permute-start.4 = (bf16[64,8192]{1,0:T(8,128)(2,1)S(1)}, bf16[64,8192]{1,0:T(8,128)(2,1)S(1)}, u32[]{:S(2)}, u32[]{:S(2)}) collective-permute-start(bf16[64,8192]{1,0:T(8,128)(2,1)S(1)} %project.5.own_ref.refs_2_), channel_id=1, source_target_pairs={{0,8},{8,0},{1,9},{9,1},{2,10},{10,2},{3,11},{11,3},{4,12},{12,4},... | collective-permute-start | bytes 3145736 | tf_op jit(solution)/shard_map/ppermute | solution.py:388
  64.9 2.8 %collective-permute-start.3 = (bf16[64,8192]{1,0:T(8,128)(2,1)S(1)}, bf16[64,8192]{1,0:T(8,128)(2,1)S(1)}, u32[]{:S(2)}, u32[]{:S(2)}) collective-permute-start(bf16[64,8192]{1,0:T(8,128)(2,1)S(1)} %project.4.own_ref.refs_3_), channel_id=1, source_target_pairs={{0,8},{8,0},{1,9},{9,1},{2,10},{10,2},{3,11},{11,3},{4,12},{12,4},... | collective-permute-start | bytes 3145736 | tf_op jit(solution)/shard_map/ppermute | solution.py:388
  68.2 3.8 %collective-permute-start.7 = (f32[32,128]{1,0:T(8,128)S(1)}, f32[32,128]{1,0:T(8,128)S(1)}, u32[]{:S(2)}, u32[]{:S(2)}) collective-permute-start(f32[32,128]{1,0:T(8,128)S(1)} %pair.7), channel_id=1, source_target_pairs={{0,1},{1,0},{2,3},{3,2},{4,5},{5,4},{6,7},{7,6},{8,9},{9,8},{10,11... | collective-permute-start | bytes 49160 | tf_op jit(solution)/shard_map/ppermute | solution.py:388
  72.0 6.0 %collective-permute-start.8 = (f32[32,128]{1,0:T(8,128)S(1)}, f32[32,128]{1,0:T(8,128)S(1)}, u32[]{:S(2)}, u32[]{:S(2)}) collective-permute-start(f32[32,128]{1,0:T(8,128)S(1)} %add.14), channel_id=1, source_target_pairs={{0,2},{1,3},{2,0},{3,1},{4,6},{5,7},{6,4},{7,5},{8,10},{9,11},{10,... | collective-permute-start | bytes 49160 | tf_op jit(solution)/shard_map/ppermute | solution.py:388
  76.2 4.7 %collective-permute-start.10 = (f32[64,64]{1,0:T(8,128)S(1)}, f32[64,64]{1,0:T(8,128)S(1)}, u32[]{:S(2)}, u32[]{:S(2)}) collective-permute-start(f32[64,64]{1,0:T(8,128)S(1)} %get-tuple-element.14.own_ref), channel_id=1, source_target_pairs={{0,8},{8,0},{1,9},{9,1},{2,10},{10,2},{3,11},{11,3},{4,12},{12,4},... | collective-permute-start | bytes 49160 | tf_op jit(solution)/shard_map/ppermute | solution.py:388
  78.0 4.7 %collective-permute-start.9 = (f32[32,128]{1,0:T(8,128)S(1)}, f32[32,128]{1,0:T(8,128)S(1)}, u32[]{:S(2)}, u32[]{:S(2)}) collective-permute-start(f32[32,128]{1,0:T(8,128)S(1)} %add.15.left_ref), channel_id=1, source_target_pairs={{0,4},{1,5},{2,6},{3,7},{4,0},{5,1},{6,2},{7,3},{8,12},{9,13},{10,... | collective-permute-start | bytes 49160 | tf_op jit(solution)/shard_map/ppermute | solution.py:388

commit v4 on v3

--- a/solution.py
+++ b/solution.py
@@ -14,6 +14,8 @@
 NT = (((1,), (1,)), ((), ()))
 TN = (((0,), (0,)), ((), ()))
 VMEM = pltpu.MemorySpace.VMEM
+EARLY = 2
+STEPS_FLOPS = 10**10
 PIECES = 4
 AHEAD = 2
 GRAM_MB, PROJ_MB, PAIR_MB, OUT_MB = 36, 12, 6, 8
@@ -49,6 +51,42 @@
     while len(terms) > 1:
         terms = [a + b for a, b in zip(terms[::2], terms[1::2])]
     return terms[0]
+
+
+def eliminate(here, cols):
+    cols = list(cols)
+    sub = iota(here.shape, 0)
+    kept = here
+    for j in range(0, 8, 2):
+        left, right = cols[j], cols[j + 1]
+        at_left, at_right = sub == j, sub == j + 1
+        pp, pq, qq = (
+            spread_lanes(left[j : j + 1]),
+            spread_lanes(right[j : j + 1]),
+            spread_lanes(right[j + 1 : j + 2]),
+        )
+        inv = 1.0 / (pp * qq - pq * pq)
+        ipp, ipq, iqq = qq * inv, -pq * inv, pp * inv
+
+        def solve(value):
+            top, low = spread_lanes(value[j : j + 1]), spread_lanes(value[j + 1 : j + 2])
+            up, down = ipp * top + ipq * low, ipq * top + iqq * low
+            rest = value - (left * up + right * down)
+            return top, low, jnp.where(at_left, up, jnp.where(at_right, down, rest))
+
+        for k in range(j + 2, len(cols)):
+            cols[k] = solve(cols[k])[2]
+        top, low, here = solve(here)
+        scale = lax.rsqrt(pp)
+        ratio = pq * scale
+        unit = top * scale
+        kept = jnp.where(at_left, unit, kept)
+        kept = jnp.where(at_right, (low - ratio * unit) * lax.rsqrt(qq - ratio * ratio), kept)
+    return kept, here, cols
+
+
+def subtract(value, cols, rows):
+    return value - pair_sum([col * row for col, row in zip(cols, rows)])
 
 
 def inverse_factor(square, zero):
@@ -58,49 +96,33 @@
     joined = jnp.where(lane < order, eye, square)
     count = order // 8
     rows = [joined[8 * b : 8 * b + 8] for b in range(count)]
-    sub = iota((8, width), 0)
+
+    def columns(row, first):
+        return [
+            spread_cols(row[:, first + j : first + j + 1], width) + zero for j in range(16)
+        ]
+
+    def spread_rows(value):
+        return [spread_lanes(value[j : j + 1]) for j in range(8)]
+
     done = []
-    for b in range(count):
-        here = rows[b]
+    for b in range(0, count, 2):
         first = order + 8 * b
-        cols = [spread_cols(here[:, first + j : first + j + 1], width) + zero for j in range(8)]
-        below = [
-            [spread_cols(rows[t][:, first + j : first + j + 1], width) for t in range(b + 1, count)]
-            for j in range(8)
+        cols, low_cols = columns(rows[b], first), columns(rows[b + 1], first)
+        below = [columns(rows[t], first) for t in range(b + 2, count)]
+        kept, high, cols = eliminate(rows[b], cols)
+        done.append(kept)
+        low = subtract(rows[b + 1], low_cols[:8], spread_rows(high))
+        next_cols = [
+            subtract(low_cols[k], low_cols[:8], spread_rows(cols[k])) for k in range(8, 16)
         ]
-        kept = here
-        for j in range(0, 8, 2):
-            left, right = cols[j], cols[j + 1]
-            at_left, at_right = sub == j, sub == j + 1
-            pp, pq, qq = (
-                spread_lanes(left[j : j + 1]),
-                spread_lanes(right[j : j + 1]),
-                spread_lanes(right[j + 1 : j + 2]),
-            )
-            inv = 1.0 / (pp * qq - pq * pq)
-            ipp, ipq, iqq = qq * inv, -pq * inv, pp * inv
-
-            def solve(value):
-                top, low = spread_lanes(value[j : j + 1]), spread_lanes(value[j + 1 : j + 2])
-                up, down = ipp * top + ipq * low, ipq * top + iqq * low
-                rest = value - (left * up + right * down)
-                return top, low, jnp.where(at_left, up, jnp.where(at_right, down, rest))
-
-            for k in range(j + 2, 8):
-                cols[k] = solve(cols[k])[2]
-            top, low, here = solve(here)
-            scale = lax.rsqrt(pp)
-            ratio = pq * scale
-            unit = top * scale
-            kept = jnp.where(at_left, unit, kept)
-            kept = jnp.where(
-                at_right, (low - ratio * unit) * lax.rsqrt(qq - ratio * ratio), kept
-            )
+        kept, low, _ = eliminate(low, next_cols)
         done.append(kept)
-        if b + 1 < count:
-            flat = [spread_lanes(here[j : j + 1]) for j in range(8)]
-            for t in range(b + 1, count):
-                rows[t] = rows[t] - pair_sum([below[j][t - b - 1] * flat[j] for j in range(8)])
+        if b + 2 < count:
+            low_rows = spread_rows(low)
+            high_rows = spread_rows(subtract(high, cols[8:], low_rows))
+            for at, t in enumerate(range(b + 2, count)):
+                rows[t] = subtract(rows[t], below[at], high_rows + low_rows)
     return jnp.where(lane < order, jnp.concatenate(done, axis=0), 0.0)
 
 
@@ -115,22 +137,45 @@
     return basis
 
 
-def unpack(packed, keep):
-    tile = lambda i: packed[:, 128 * i : 128 * i + 128]
+def assemble(square, cross, corner):
+    low = jnp.concatenate([cross, corner], axis=1)
+    size = square.shape[0]
+    pad = jnp.zeros((128 - cross.shape[0], size), F32)
+    top = jnp.concatenate([square, jnp.concatenate([cross, pad], axis=0).T], axis=1)
+    return jnp.concatenate([top, low, jnp.zeros_like(low)], axis=0)
+
+
+def prior_block(mixed):
+    keep = mixed.shape[0]
+    lane, row = iota(mixed.shape, 1), iota(mixed.shape, 0)
+    turned = jnp.concatenate([mixed, mixed], axis=0).T[:keep]
+    return jnp.where(lane < keep, jnp.where(row <= lane, mixed, turned), 0.0)
+
+
+def unpack_early(early):
+    mixed = early[:, 256:384]
+    upper = jnp.concatenate([early[:, 0:128], mixed], axis=0)
+    square = jnp.where(iota(upper.shape, 0) <= iota(upper.shape, 1), upper, upper.T)
+    return assemble(square, early[:, 128:256], prior_block(mixed))
+
+
+def unpack(early, late):
+    keep = early.shape[0]
+    tile = lambda i: late[:, 128 * i : 128 * i + 128]
     lane, row = iota((keep, 128), 1), iota((keep, 128), 0)
     zero = jnp.zeros((keep, 128), F32)
-    mixed = tile(6)
+    first, mixed = early[:, 0:128], early[:, 256:384]
     diag = jnp.where(
         lane == 127,
         pltpu.roll(jnp.broadcast_to(mixed[keep - 2 : keep - 1], mixed.shape), 127, 1),
         pltpu.roll(jnp.broadcast_to(mixed[keep - 1 : keep], mixed.shape), keep, 1),
     )
-    end = jnp.where(lane == row + keep, diag, pltpu.roll(tile(0), keep, 1))
+    end = jnp.where(lane == row + keep, diag, pltpu.roll(first, keep, 1))
     upper = jnp.concatenate(
         [
-            jnp.concatenate([tile(0), tile(1)], axis=1),
-            jnp.concatenate([mixed, tile(2)], axis=1),
-            jnp.concatenate([zero, tile(3)], axis=1),
+            jnp.concatenate([first, tile(0)], axis=1),
+            jnp.concatenate([mixed, tile(1)], axis=1),
+            jnp.concatenate([zero, tile(2)], axis=1),
             jnp.concatenate([zero, end], axis=1),
         ],
         axis=0,
@@ -141,66 +186,91 @@
     held = ((high <= wide) & (wide < last)) | ((high < last) & (wide >= last))
     held |= (high >= wide) & (high >= last) & (wide >= last)
     square = jnp.where(held, upper, upper.T)
-    cross = jnp.concatenate([tile(4), tile(5)], axis=1)
-    turned = jnp.concatenate([mixed, mixed], axis=0).T[:keep]
-    corner = jnp.where(lane < keep, jnp.where(row <= lane, mixed, turned), 0.0)
-    low = jnp.concatenate([cross, corner], axis=1)
-    cross_pad = jnp.concatenate([cross, jnp.zeros_like(cross)], axis=0)
-    top = jnp.concatenate([square, cross_pad.T], axis=1)
-    return jnp.concatenate([top, low, jnp.zeros_like(low)], axis=0)
+    cross = jnp.concatenate([early[:, 128:256], tile(3)], axis=1)
+    return assemble(square, cross, prior_block(mixed))
 
 
 def trace(gram):
     return jnp.sum(jnp.where(iota(gram.shape, 0) == iota(gram.shape, 1), gram, 0.0))
 
 
-def steps_kernel(left_ref, right_ref, out_ref, modes_ref, total_ref, both_ref, zero_ref):
-    keep = left_ref.shape[0]
-    zero_ref[...] = jnp.zeros_like(zero_ref)
-    total = unpack(left_ref[...] + right_ref[...], keep)
-    scale = trace(total)
-    total = total * (1.0 / scale)
-    total_ref[...] = total
-    width = total.shape[0]
-    frames = STEPS * keep
+def run_steps(first, last, keep, total_ref, both_ref, zero):
+    width = total_ref.shape[0]
     shape = (keep, width)
-    both_ref[:keep, :width] = total[frames : frames + keep]
-    both_ref[:keep, width:] = (iota(shape, 1) == iota(shape, 0) + frames).astype(F32)
-
-    @pl.loop(0, STEPS)
+
+    @pl.loop(first, last)
     def _(step):
         at = pl.multiple_of(step * keep, keep)
         both_ref[keep:, :width] = total_ref[pl.ds(at, keep)]
         both_ref[keep:, width:] = (iota(shape, 1) == iota(shape, 0) + at).astype(F32)
         both = both_ref[...]
         gram = dot(both[:, :width], both[:, width:], NT)
-        both_ref[:keep] = dot(basis_rows(gram, keep, zero_ref[...]), both)
-
+        both_ref[:keep] = dot(basis_rows(gram, keep, zero), both)
+
+
+def early_kernel(left_ref, right_ref, out_ref, total_ref, both_ref, zero_ref):
+    keep = left_ref.shape[0]
+    zero_ref[...] = jnp.zeros_like(zero_ref)
+    total = unpack_early(left_ref[...] + right_ref[...])
+    total = total * (1.0 / trace(total))
+    total_ref[...] = total
+    width = total.shape[0]
+    frames = EARLY * keep
+    shape = (keep, width)
+    both_ref[:keep, :width] = total[frames : frames + keep]
+    both_ref[:keep, width:] = (iota(shape, 1) == iota(shape, 0) + frames).astype(F32)
+    run_steps(0, EARLY, keep, total_ref, both_ref, zero_ref[...])
+    out_ref[...] = both_ref[:keep, width:]
+
+
+def late_kernel(
+    left_ref, right_ref, late_left, late_right, before_ref, out_ref, modes_ref, total_ref, both_ref, zero_ref
+):
+    keep = left_ref.shape[0]
+    zero_ref[...] = jnp.zeros_like(zero_ref)
+    total = unpack(left_ref[...] + right_ref[...], late_left[...] + late_right[...])
+    scale = trace(total)
+    total = total * (1.0 / scale)
+    total_ref[...] = total
+    width = total.shape[0]
+    before = before_ref[...]
+    fresh = EARLY * keep
+    gap = jnp.zeros((keep, (STEPS - EARLY) * keep), F32)
+    weights = jnp.concatenate([before[:, :fresh], gap, before[:, fresh:]], axis=1)
+    both_ref[:keep, :width] = dot(weights, total)
+    both_ref[:keep, width:] = weights
+    run_steps(EARLY, STEPS, keep, total_ref, both_ref, zero_ref[...])
     out_ref[...] = both_ref[:keep, width:]
     modes_ref[...] = dot(both_ref[:keep, :width], both_ref[:keep, width:], NT) * scale
 
 
-def steps_weights(left, right, keep):
+def steps_weights(early, late, keep):
+    def call(kernel, shapes, width, *args):
+        return pl.pallas_call(
+            kernel,
+            out_shape=tuple(jax.ShapeDtypeStruct(shape, F32) for shape in shapes),
+            in_specs=[pl.BlockSpec(memory_space=VMEM)] * len(args),
+            out_specs=tuple(pl.BlockSpec(memory_space=VMEM) for shape in shapes),
+            scratch_shapes=[
+                pltpu.VMEM((width, width), F32),
+                pltpu.VMEM((2 * keep, 2 * width), F32),
+                pltpu.VMEM((8, 2 * keep), F32),
+            ],
+            name="steps",
+            compiler_params=grant(6),
+            cost_estimate=pl.CostEstimate(
+                flops=STEPS_FLOPS, bytes_accessed=1 << 20, transcendentals=0
+            ),
+        )(*args)
+
+    (before,) = call(early_kernel, [(keep, (EARLY + 2) * keep)], (EARLY + 2) * keep, *early)
     width = (STEPS + 2) * keep
-    return pl.pallas_call(
-        steps_kernel,
-        out_shape=(
-            jax.ShapeDtypeStruct((keep, width), F32),
-            jax.ShapeDtypeStruct((keep, keep), F32),
-        ),
-        in_specs=[pl.BlockSpec(memory_space=VMEM)] * 2,
-        out_specs=[pl.BlockSpec(memory_space=VMEM)] * 2,
-        scratch_shapes=[
-            pltpu.VMEM((width, width), F32),
-            pltpu.VMEM((2 * keep, 2 * width), F32),
-            pltpu.VMEM((8, 2 * keep), F32),
-        ],
-        name="steps",
-        compiler_params=grant(6),
-    )(left, right)
-
-
-def gram_kernel(cuts, prior_in, frames_in, out_ref, prior_ref, frames_ref, sems, square_ref, corner_ref):
+    return call(late_kernel, [(keep, width), (keep, keep)], width, *early, *late, before)
+
+
+def gram_kernel(
+    cuts, prior_in, frames_in, early_ref, late_ref, prior_ref, frames_ref, sems, square_ref, corner_ref
+):
     keep = prior_ref.shape[0]
     blocks = [slice(low, high) for low, high in zip(cuts[:-1], cuts[1:])]
 
@@ -237,12 +307,13 @@
     mixed = jnp.where((row == keep - 1) & (lane < keep - 1), pltpu.roll(diag, keep, 1), mixed)
     mixed = jnp.where((row == keep - 2) & (lane == 0), pltpu.roll(diag, 1, 1), mixed)
     free = (lane < keep) & (row > lane)
-    out_ref[:, 0:128] = jnp.where(free, pltpu.roll(end, keep, 1), square_ref[0:64, 0:128])
-    out_ref[:, 128:256] = square_ref[0:64, 128:256]
-    out_ref[:, 256:384] = square_ref[64:128, 128:256]
-    out_ref[:, 384:512] = square_ref[128:192, 128:256]
-    out_ref[:, 512:768] = square_ref[256:320]
-    out_ref[:, 768:896] = mixed
+    early_ref[:, 0:128] = jnp.where(free, pltpu.roll(end, keep, 1), square_ref[0:64, 0:128])
+    early_ref[:, 128:256] = square_ref[256:320, 0:128]
+    early_ref[:, 256:384] = mixed
+    late_ref[:, 0:128] = square_ref[0:64, 128:256]
+    late_ref[:, 128:256] = square_ref[64:128, 128:256]
+    late_ref[:, 256:384] = square_ref[128:192, 128:256]
+    late_ref[:, 384:512] = square_ref[256:320, 128:256]
 
 
 def local_gram(prior_t, frames, cuts):
@@ -251,12 +322,13 @@
     return pl.pallas_call(
         functools.partial(gram_kernel, cuts),
         out_shape=(
-            jax.ShapeDtypeStruct((keep, 14 * keep), F32),
+            pltpu.VMEM((keep, 6 * keep), F32),
+            pltpu.VMEM((keep, 8 * keep), F32),
             pltpu.VMEM(prior_t.shape, prior_t.dtype),
             pltpu.VMEM(frames.shape, frames.dtype),
         ),
         in_specs=[pl.BlockSpec(memory_space=pltpu.MemorySpace.HBM)] * 2,
-        out_specs=[pl.BlockSpec(memory_space=VMEM)] * 3,
+        out_specs=[pl.BlockSpec(memory_space=VMEM)] * 4,
         scratch_shapes=[
             pltpu.SemaphoreType.DMA((2, len(cuts) - 1)),
             pltpu.VMEM((width + keep, width), F32),
@@ -413,8 +485,9 @@
 def shards(prior, snapshots):
     keep = prior.shape[2]
     rows = prior.shape[1]
-    local, prior_t, frames = local_gram(prior[0].T, snapshots[0], cuts_of(rows))
-    weights, own_gram = steps_weights(*all_but_last_sum(local, "rows", True), keep)
+    early, late, prior_t, frames = local_gram(prior[0].T, snapshots[0], cuts_of(rows))
+    early, late = (all_but_last_sum(part, "rows", True) for part in (early, late))
+    weights, own_gram = steps_weights(early, late, keep)
     other_gram = flip(own_gram, "tm", 1)
     piece = rows // PIECES
     owns, others = [], []

time: 89.8 us -> 82.9 us (0.923)
  waiting for transfers between devices: 21.6 us -> 12.5 us
  starting transfers between devices: 18.5 us -> 23.8 us
  Pallas kernels: 48.3 us -> 46.1 us
  other arithmetic: 1 us -> 0.07 us
    ppermute x11 -> x14, waiting for transfers between devices: 21.6 us -> 12.5 us  [flip(): return lax.ppermute(block, axis, [(i, i ^ mask) for i in range(count)])]
    ppermute x11 -> x14, starting transfers between devices: 18.5 us -> 23.8 us  [flip(): return lax.ppermute(block, axis, [(i, i ^ mask) for i in range(count)])]
    pallas_call x2 -> x3, Pallas kernels: 34.2 us -> 32.4 us  [the longest x2 19.9 us: call(): pl.pallas_call(kernel, out_shape=tuple((jax.ShapeDtypeStruct(shape, F32)...]
    add x4 -> x6, other arithmetic: 1 us -> 0.07 us  [all_but_last_sum(): value = value + flip(value, axis, mask)]
  transfers between devices with their start and end apart: 11 -> 14, of which waited for: 7 -> 7; matrix products, arithmetic and copies ran while one was open for 0% -> 0% of each run, Pallas kernels for 6% -> 18%
where the time goes in v4:
time: 82.9 us; the launch traced here: 82.8 us
  Pallas kernels  46.1 us (56%)
  starting transfers between devices  23.8 us (29%)
  waiting for transfers between devices  12.5 us (15%)
    ppermute x14, starting transfers between devices, flip(): return lax.ppermute(block, axis, [(i, i ^ mask) for i in range(count)])  23.8 us
    pallas_call x2, Pallas kernels, call(): pl.pallas_call(kernel, out_shape=tuple((jax.ShapeDtypeStruct(shape, F32)...  19.9 us
    pallas_call x1, Pallas kernels, local_gram(): pl.pallas_call(functools.partial(gram_kernel, cuts), out_shape=(pltpu.VME...  12.5 us
    ppermute x14, waiting for transfers between devices, flip(): return lax.ppermute(block, axis, [(i, i ^ mask) for i in range(count)])  12.5 us
    pallas_call x4, Pallas kernels, project(): pl.pallas_call(functools.partial(modes_kernel, first), out_shape=pltpu.VM...  5.38 us
    pallas_call x1, Pallas kernels, merge_weights(): pl.pallas_call(merge_kernel, out_shape=jax.ShapeDtypeStruct((keep // 2, 2...  4.27 us
    pallas_call x1, Pallas kernels, output(): pl.pallas_call(functools.partial(output_kernel, len(owns)), out_shape=jax...  2.15 us
    pallas_call x4, Pallas kernels, pair_gram(): pl.pallas_call(pair_kernel, out_shape=jax.ShapeDtypeStruct((keep // 2, 2...  1.93 us
  transfers between devices with their start and end apart: 14, of which 7 were waited for; matrix products, arithmetic and copies ran while one was open for 0% of the time, Pallas kernels for 18%

profile of v4, /device:TPU:0, one launch (start us, length us, event | category | flops | bytes accessed | tf_op | source)
XLA Modules:
  0.0 82.8 jit_solution(9306709712675469822)
XLA Ops:
  0.0 12.5 %gram.1 = (f32[64,384]{1,0:T(8,128)S(1)}, f32[64,512]{1,0:T(8,128)S(1)}, bf16[64,32768]{1,0:T(8,128)(2,1)S(1)}, bf16[32768,256]{1,0:T(8,128)(2,1)S(1)}) custom-call(bf16[64,32768]{1,0:T(8,128)(2,1)} %bitcast.6, bf16[32768,256]{1,0:T(8,128)(2,1)} %bitcast.5), custom_call_target="tpu_custom_call" | custom-call | tf_op jit(solution)/shard_map/gram/pallas_call | solution.py:322
  12.6 3.1 %collective-permute-start = (f32[64,384]{1,0:T(8,128)S(1)}, f32[64,384]{1,0:T(8,128)S(1)}, u32[]{:S(2)}, u32[]{:S(2)}) collective-permute-start(f32[64,384]{1,0:T(8,128)S(1)} %get-tuple-element.11), channel_id=1, source_target_pairs={{0,1},{1,0},{2,3},{3,2},{4,5},{5,4},{6,7},{7,6},{8,9},{9,8},{10,11... | collective-permute-start | bytes 294920 | tf_op jit(solution)/shard_map/ppermute | solution.py:460
  15.6 0.1 collective-permute-start.3
  15.7 3.3 %collective-permute-done = f32[64,384]{1,0:T(8,128)S(1)} collective-permute-done((f32[64,384]{1,0:T(8,128)S(1)}, f32[64,384]{1,0:T(8,128)S(1)}, u32[]{:S(2)}, u32[]{:S(2)}) %collective-permute-start) | collective-permute-done | bytes 98336 | tf_op jit(solution)/shard_map/ppermute | solution.py:460
  19.1 2.3 %collective-permute-start.1 = (f32[64,384]{1,0:T(8,128)S(1)}, f32[64,384]{1,0:T(8,128)S(1)}, u32[]{:S(2)}, u32[]{:S(2)}) collective-permute-start(f32[64,384]{1,0:T(8,128)S(1)} %add.18), channel_id=1, source_target_pairs={{0,2},{1,3},{2,0},{3,1},{4,6},{5,7},{6,4},{7,5},{8,10},{9,11},{10,... | collective-permute-start | bytes 294920 | tf_op jit(solution)/shard_map/ppermute | solution.py:460
  21.3 1.8 %collective-permute-start.4 = (f32[64,512]{1,0:T(8,128)S(1)}, f32[64,512]{1,0:T(8,128)S(1)}, u32[]{:S(2)}, u32[]{:S(2)}) collective-permute-start(f32[64,512]{1,0:T(8,128)S(1)} %add.20), channel_id=1, source_target_pairs={{0,2},{1,3},{2,0},{3,1},{4,6},{5,7},{6,4},{7,5},{8,10},{9,11},{10,... | collective-permute-start | bytes 393224 | tf_op jit(solution)/shard_map/ppermute | solution.py:460
  23.2 1.4 %collective-permute-done.1 = f32[64,384]{1,0:T(8,128)S(1)} collective-permute-done((f32[64,384]{1,0:T(8,128)S(1)}, f32[64,384]{1,0:T(8,128)S(1)}, u32[]{:S(2)}, u32[]{:S(2)}) %collective-permute-start.1) | collective-permute-done | bytes 98336 | tf_op jit(solution)/shard_map/ppermute | solution.py:460
  24.6 4.4 %collective-permute-start.2 = (f32[64,384]{1,0:T(8,128)S(1)}, f32[64,384]{1,0:T(8,128)S(1)}, u32[]{:S(2)}, u32[]{:S(2)}) collective-permute-start(f32[64,384]{1,0:T(8,128)S(1)} %add.19.left_ref), channel_id=1, source_target_pairs={{0,6},{1,7},{2,4},{3,5},{4,2},{5,3},{6,0},{7,1},{8,14},{9,15},{10,... | collective-permute-start | bytes 294920 | tf_op jit(solution)/shard_map/ppermute | solution.py:460
  29.0 2.9 %collective-permute-start.5 = (f32[64,512]{1,0:T(8,128)S(1)}, f32[64,512]{1,0:T(8,128)S(1)}, u32[]{:S(2)}, u32[]{:S(2)}) collective-permute-start(f32[64,512]{1,0:T(8,128)S(1)} %add.21.late_left), channel_id=1, source_target_pairs={{0,6},{1,7},{2,4},{3,5},{4,2},{5,3},{6,0},{7,1},{8,14},{9,15},{10,... | collective-permute-start | bytes 393224 | tf_op jit(solution)/shard_map/ppermute | solution.py:460
  31.9 0.3 collective-permute-done.2.right_ref
  32.2 9.3 %steps.2.before_ref = f32[64,256]{1,0:T(8,128)S(1)} custom-call(f32[64,384]{1,0:T(8,128)S(1)} %add.19.left_ref, f32[64,384]{1,0:T(8,128)S(1)} %collective-permute-done.2.right_ref), custom_call_target="tpu_custom_call" | custom-call | flops 10000000000 | bytes 1048576 | tf_op jit(solution)/shard_map/steps/pallas_call | solution.py:249
  41.5 10.6 %steps.3 = (f32[64,384]{1,0:T(8,128)S(1)}, f32[64,64]{1,0:T(8,128)S(1)}) custom-call(f32[64,384]{1,0:T(8,128)S(1)} %add.19.left_ref, f32[64,384]{1,0:T(8,128)S(1)} %collective-permute-done.2.right_ref, f32[64,512]{1,0:T(8,128)S(1)} %add.21.late_left, f32[64,512]{1,0:T(8,128)S(1)} %collective-permute-done.5.late_right, f32[64,256]{1,0:T(8,128)S(1)} %steps.2.before_ref), custom_call_target="tpu_custom_call" | custom-call | flops 10000000000 | bytes 1048576 | tf_op jit(solution)/shard_map/steps/pallas_call | solution.py:249
  52.1 1.3 %project.7.own_ref.refs_0_ = bf16[64,8192]{1,0:T(8,128)(2,1)S(1)} custom-call(f32[64,384]{1,0:T(8,128)S(1)} %get-tuple-element.13.weights_ref, bf16[64,32768]{1,0:T(8,128)(2,1)S(1)} %get-tuple-element.14.prior_ref, bf16[32768,256]{1,0:T(8,128)(2,1)S(1)} %get-tuple-element.15.frames_ref), custom_call_target="tpu_custom_call" | custom-call | tf_op jit(solution)/shard_map/project/pallas_call | solution.py:362
  53.5 1.3 %project.6.own_ref.refs_1_ = bf16[64,8192]{1,0:T(8,128)(2,1)S(1)} custom-call(f32[64,384]{1,0:T(8,128)S(1)} %get-tuple-element.13.weights_ref, bf16[64,32768]{1,0:T(8,128)(2,1)S(1)} %get-tuple-element.14.prior_ref, bf16[32768,256]{1,0:T(8,128)(2,1)S(1)} %get-tuple-element.15.frames_ref), custom_call_target="tpu_custom_call" | custom-call | tf_op jit(solution)/shard_map/project/pallas_call | solution.py:362
  54.9 0.6 collective-permute-start.8
  55.4 1.3 %project.5.own_ref.refs_2_ = bf16[64,8192]{1,0:T(8,128)(2,1)S(1)} custom-call(f32[64,384]{1,0:T(8,128)S(1)} %get-tuple-element.13.weights_ref, bf16[64,32768]{1,0:T(8,128)(2,1)S(1)} %get-tuple-element.14.prior_ref, bf16[32768,256]{1,0:T(8,128)(2,1)S(1)} %get-tuple-element.15.frames_ref), custom_call_target="tpu_custom_call" | custom-call | tf_op jit(solution)/shard_map/project/pallas_call | solution.py:362
  56.8 0.1 collective-permute-start.7
  56.9 1.3 %project.4.own_ref.refs_3_ = bf16[64,8192]{1,0:T(8,128)(2,1)S(1)} custom-call(f32[64,384]{1,0:T(8,128)S(1)} %get-tuple-element.13.weights_ref, bf16[64,32768]{1,0:T(8,128)(2,1)S(1)} %get-tuple-element.14.prior_ref, bf16[32768,256]{1,0:T(8,128)(2,1)S(1)} %get-tuple-element.15.frames_ref), custom_call_target="tpu_custom_call" | custom-call | tf_op jit(solution)/shard_map/project/pallas_call | solution.py:362
  58.2 0.6 collective-permute-start.6
  58.8 0.5 pair.4.rest_0_
  59.3 0.5 pair.5.rest_0_
  59.8 0.5 pair.6.rest_0_
  60.2 0.8 collective-permute-done.6.other_ref.refs_7_
  61.1 0.5 pair.7
  61.5 2.2 %collective-permute-start.10 = (f32[32,128]{1,0:T(8,128)S(1)}, f32[32,128]{1,0:T(8,128)S(1)}, u32[]{:S(2)}, u32[]{:S(2)}) collective-permute-start(f32[32,128]{1,0:T(8,128)S(1)} %pair.7), channel_id=1, source_target_pairs={{0,1},{1,0},{2,3},{3,2},{4,5},{5,4},{6,7},{7,6},{8,9},{9,8},{10,11... | collective-permute-start | bytes 49160 | tf_op jit(solution)/shard_map/ppermute | solution.py:460
  63.7 1.7 %collective-permute-done.10 = f32[32,128]{1,0:T(8,128)S(1)} collective-permute-done((f32[32,128]{1,0:T(8,128)S(1)}, f32[32,128]{1,0:T(8,128)S(1)}, u32[]{:S(2)}, u32[]{:S(2)}) %collective-permute-start.10) | collective-permute-done | bytes 16416 | tf_op jit(solution)/shard_map/ppermute | solution.py:460
  65.4 4.4 %collective-permute-start.11 = (f32[32,128]{1,0:T(8,128)S(1)}, f32[32,128]{1,0:T(8,128)S(1)}, u32[]{:S(2)}, u32[]{:S(2)}) collective-permute-start(f32[32,128]{1,0:T(8,128)S(1)} %add.22), channel_id=1, source_target_pairs={{0,2},{1,3},{2,0},{3,1},{4,6},{5,7},{6,4},{7,5},{8,10},{9,11},{10,... | collective-permute-start | bytes 49160 | tf_op jit(solution)/shard_map/ppermute | solution.py:460
  69.8 1.7 %collective-permute-done.11 = f32[32,128]{1,0:T(8,128)S(1)} collective-permute-done((f32[32,128]{1,0:T(8,128)S(1)}, f32[32,128]{1,0:T(8,128)S(1)}, u32[]{:S(2)}, u32[]{:S(2)}) %collective-permute-start.11) | collective-permute-done | bytes 16416 | tf_op jit(solution)/shard_map/ppermute | solution.py:460
  71.5 1.5 %collective-permute-start.12 = (f32[32,128]{1,0:T(8,128)S(1)}, f32[32,128]{1,0:T(8,128)S(1)}, u32[]{:S(2)}, u32[]{:S(2)}) collective-permute-start(f32[32,128]{1,0:T(8,128)S(1)} %add.23.left_ref), channel_id=1, source_target_pairs={{0,4},{1,5},{2,6},{3,7},{4,0},{5,1},{6,2},{7,3},{8,12},{9,13},{10,... | collective-permute-start | bytes 49160 | tf_op jit(solution)/shard_map/ppermute | solution.py:460
  73.0 3.2 %collective-permute-done.12.right_ref = f32[32,128]{1,0:T(8,128)S(1)} collective-permute-done((f32[32,128]{1,0:T(8,128)S(1)}, f32[32,128]{1,0:T(8,128)S(1)}, u32[]{:S(2)}, u32[]{:S(2)}) %collective-permute-start.12) | collective-permute-done | bytes 16416 | tf_op jit(solution)/shard_map/ppermute | solution.py:460
  76.2 4.3 %merge.1.weights_ref = f32[32,128]{1,0:T(8,128)S(1)} custom-call(f32[32,128]{1,0:T(8,128)S(1)} %add.23.left_ref, f32[32,128]{1,0:T(8,128)S(1)} %collective-permute-done.12.right_ref, f32[64,64]{1,0:T(8,128)S(1)} %get-tuple-element.16.own_ref, f32[64,64]{1,0:T(8,128)S(1)} %collective-permute-done.13.other_ref), custom_call_target="tpu_custom_call" | custom-call | tf_op jit(solution)/shard_map/merge/pallas_call | solution.py:414
  80.4 2.2 %output.1 = bf16[32,32768]{1,0:T(8,128)(2,1)} custom-call(f32[32,128]{1,0:T(8,128)S(1)} %merge.1.weights_ref, bf16[64,8192]{1,0:T(8,128)(2,1)S(1)} %project.7.own_ref.refs_0_, bf16[64,8192]{1,0:T(8,128)(2,1)S(1)} %project.6.own_ref.refs_1_, bf16[64,8192]{1,0:T(8,128)(2,1)S(1)} %project.5.own_ref.refs_2_, bf16[64,8192]{1,0:T(8,128)(2,1)S(1)} %project.4.own_ref.refs_3_, ...), custom_call_target="tpu_custom_call" | custom-call | tf_op jit(solution)/shard_map/output/pallas_call | solution.py:447
  (15 shorter events, 0.2 us)
Async XLA Ops:
  12.6 6.5 %collective-permute-start = (f32[64,384]{1,0:T(8,128)S(1)}, f32[64,384]{1,0:T(8,128)S(1)}, u32[]{:S(2)}, u32[]{:S(2)}) collective-permute-start(f32[64,384]{1,0:T(8,128)S(1)} %get-tuple-element.11), channel_id=1, source_target_pairs={{0,1},{1,0},{2,3},{3,2},{4,5},{5,4},{6,7},{7,6},{8,9},{9,8},{10,11... | collective-permute-start | bytes 294920 | tf_op jit(solution)/shard_map/ppermute | solution.py:460
  15.6 5.7 %collective-permute-start.3 = (f32[64,512]{1,0:T(8,128)S(1)}, f32[64,512]{1,0:T(8,128)S(1)}, u32[]{:S(2)}, u32[]{:S(2)}) collective-permute-start(f32[64,512]{1,0:T(8,128)S(1)} %get-tuple-element.12), channel_id=1, source_target_pairs={{0,1},{1,0},{2,3},{3,2},{4,5},{5,4},{6,7},{7,6},{8,9},{9,8},{10,11... | collective-permute-start | bytes 393224 | tf_op jit(solution)/shard_map/ppermute | solution.py:460
  19.1 5.5 %collective-permute-start.1 = (f32[64,384]{1,0:T(8,128)S(1)}, f32[64,384]{1,0:T(8,128)S(1)}, u32[]{:S(2)}, u32[]{:S(2)}) collective-permute-start(f32[64,384]{1,0:T(8,128)S(1)} %add.18), channel_id=1, source_target_pairs={{0,2},{1,3},{2,0},{3,1},{4,6},{5,7},{6,4},{7,5},{8,10},{9,11},{10,... | collective-permute-start | bytes 294920 | tf_op jit(solution)/shard_map/ppermute | solution.py:460
  21.3 7.7 %collective-permute-start.4 = (f32[64,512]{1,0:T(8,128)S(1)}, f32[64,512]{1,0:T(8,128)S(1)}, u32[]{:S(2)}, u32[]{:S(2)}) collective-permute-start(f32[64,512]{1,0:T(8,128)S(1)} %add.20), channel_id=1, source_target_pairs={{0,2},{1,3},{2,0},{3,1},{4,6},{5,7},{6,4},{7,5},{8,10},{9,11},{10,... | collective-permute-start | bytes 393224 | tf_op jit(solution)/shard_map/ppermute | solution.py:460
  24.6 7.6 %collective-permute-start.2 = (f32[64,384]{1,0:T(8,128)S(1)}, f32[64,384]{1,0:T(8,128)S(1)}, u32[]{:S(2)}, u32[]{:S(2)}) collective-permute-start(f32[64,384]{1,0:T(8,128)S(1)} %add.19.left_ref), channel_id=1, source_target_pairs={{0,6},{1,7},{2,4},{3,5},{4,2},{5,3},{6,0},{7,1},{8,14},{9,15},{10,... | collective-permute-start | bytes 294920 | tf_op jit(solution)/shard_map/ppermute | solution.py:460
  29.0 12.5 %collective-permute-start.5 = (f32[64,512]{1,0:T(8,128)S(1)}, f32[64,512]{1,0:T(8,128)S(1)}, u32[]{:S(2)}, u32[]{:S(2)}) collective-permute-start(f32[64,512]{1,0:T(8,128)S(1)} %add.21.late_left), channel_id=1, source_target_pairs={{0,6},{1,7},{2,4},{3,5},{4,2},{5,3},{6,0},{7,1},{8,14},{9,15},{10,... | collective-permute-start | bytes 393224 | tf_op jit(solution)/shard_map/ppermute | solution.py:460
  53.4 5.3 %collective-permute-start.9 = (bf16[64,8192]{1,0:T(8,128)(2,1)S(1)}, bf16[64,8192]{1,0:T(8,128)(2,1)S(1)}, u32[]{:S(2)}, u32[]{:S(2)}) collective-permute-start(bf16[64,8192]{1,0:T(8,128)(2,1)S(1)} %project.7.own_ref.refs_0_), channel_id=1, source_target_pairs={{0,8},{8,0},{1,9},{9,1},{2,10},{10,2},{3,11},{11,3},{4,12},{12,4},... | collective-permute-start | bytes 3145736 | tf_op jit(solution)/shard_map/ppermute | solution.py:460
  54.9 4.4 %collective-permute-start.8 = (bf16[64,8192]{1,0:T(8,128)(2,1)S(1)}, bf16[64,8192]{1,0:T(8,128)(2,1)S(1)}, u32[]{:S(2)}, u32[]{:S(2)}) collective-permute-start(bf16[64,8192]{1,0:T(8,128)(2,1)S(1)} %project.6.own_ref.refs_1_), channel_id=1, source_target_pairs={{0,8},{8,0},{1,9},{9,1},{2,10},{10,2},{3,11},{11,3},{4,12},{12,4},... | collective-permute-start | bytes 3145736 | tf_op jit(solution)/shard_map/ppermute | solution.py:460
  56.8 3.0 %collective-permute-start.7 = (bf16[64,8192]{1,0:T(8,128)(2,1)S(1)}, bf16[64,8192]{1,0:T(8,128)(2,1)S(1)}, u32[]{:S(2)}, u32[]{:S(2)}) collective-permute-start(bf16[64,8192]{1,0:T(8,128)(2,1)S(1)} %project.5.own_ref.refs_2_), channel_id=1, source_target_pairs={{0,8},{8,0},{1,9},{9,1},{2,10},{10,2},{3,11},{11,3},{4,12},{12,4},... | collective-permute-start | bytes 3145736 | tf_op jit(solution)/shard_map/ppermute | solution.py:460
  58.2 2.8 %collective-permute-start.6 = (bf16[64,8192]{1,0:T(8,128)(2,1)S(1)}, bf16[64,8192]{1,0:T(8,128)(2,1)S(1)}, u32[]{:S(2)}, u32[]{:S(2)}) collective-permute-start(bf16[64,8192]{1,0:T(8,128)(2,1)S(1)} %project.4.own_ref.refs_3_), channel_id=1, source_target_pairs={{0,8},{8,0},{1,9},{9,1},{2,10},{10,2},{3,11},{11,3},{4,12},{12,4},... | collective-permute-start | bytes 3145736 | tf_op jit(solution)/shard_map/ppermute | solution.py:460
  61.5 3.9 %collective-permute-start.10 = (f32[32,128]{1,0:T(8,128)S(1)}, f32[32,128]{1,0:T(8,128)S(1)}, u32[]{:S(2)}, u32[]{:S(2)}) collective-permute-start(f32[32,128]{1,0:T(8,128)S(1)} %pair.7), channel_id=1, source_target_pairs={{0,1},{1,0},{2,3},{3,2},{4,5},{5,4},{6,7},{7,6},{8,9},{9,8},{10,11... | collective-permute-start | bytes 49160 | tf_op jit(solution)/shard_map/ppermute | solution.py:460
  65.4 6.1 %collective-permute-start.11 = (f32[32,128]{1,0:T(8,128)S(1)}, f32[32,128]{1,0:T(8,128)S(1)}, u32[]{:S(2)}, u32[]{:S(2)}) collective-permute-start(f32[32,128]{1,0:T(8,128)S(1)} %add.22), channel_id=1, source_target_pairs={{0,2},{1,3},{2,0},{3,1},{4,6},{5,7},{6,4},{7,5},{8,10},{9,11},{10,... | collective-permute-start | bytes 49160 | tf_op jit(solution)/shard_map/ppermute | solution.py:460
  69.8 3.2 %collective-permute-start.13 = (f32[64,64]{1,0:T(8,128)S(1)}, f32[64,64]{1,0:T(8,128)S(1)}, u32[]{:S(2)}, u32[]{:S(2)}) collective-permute-start(f32[64,64]{1,0:T(8,128)S(1)} %get-tuple-element.16.own_ref), channel_id=1, source_target_pairs={{0,8},{8,0},{1,9},{9,1},{2,10},{10,2},{3,11},{11,3},{4,12},{12,4},... | collective-permute-start | bytes 49160 | tf_op jit(solution)/shard_map/ppermute | solution.py:460
  71.5 4.6 %collective-permute-start.12 = (f32[32,128]{1,0:T(8,128)S(1)}, f32[32,128]{1,0:T(8,128)S(1)}, u32[]{:S(2)}, u32[]{:S(2)}) collective-permute-start(f32[32,128]{1,0:T(8,128)S(1)} %add.23.left_ref), channel_id=1, source_target_pairs={{0,4},{1,5},{2,6},{3,7},{4,0},{5,1},{6,2},{7,3},{8,12},{9,13},{10,... | collective-permute-start | bytes 49160 | tf_op jit(solution)/shard_map/ppermute | solution.py:460

commit v5 on v4

--- a/solution.py
+++ b/solution.py
@@ -460,14 +460,25 @@
     return lax.ppermute(block, axis, [(i, i ^ mask) for i in range(count)])
 
 
-def all_but_last_sum(value, axis, mirror):
-    count = lax.axis_size(axis)
-    masks = [1 << bit for bit in range(count.bit_length() - 1)]
+def hop(block, masks):
+    count = lax.axis_size("rows")
+    route = [
+        (t * count + i, t * count + (i ^ mask)) for t, mask in enumerate(masks) for i in range(count)
+    ]
+    return lax.ppermute(block, ("tm", "rows"), route)
+
+
+def all_but_last_sum(value, mirror):
+    bits = lax.axis_size("rows").bit_length() - 1
+    masks = [1 << bit for bit in range(bits)]
     if mirror:
         masks = masks[:1] + [2 * mask - 2 for mask in masks[1:]]
-    for mask in masks[:-1]:
-        value = value + flip(value, axis, mask)
-    return value, flip(value, axis, masks[-1])
+    hops = [
+        [masks[(at + t) % bits] for t in range(lax.axis_size("tm"))] for at in range(bits)
+    ]
+    for step in hops[:-1]:
+        value = value + hop(value, step)
+    return value, hop(value, hops[-1])
 
 
 def cuts_of(rows):
@@ -486,7 +497,7 @@
     keep = prior.shape[2]
     rows = prior.shape[1]
     early, late, prior_t, frames = local_gram(prior[0].T, snapshots[0], cuts_of(rows))
-    early, late = (all_but_last_sum(part, "rows", True) for part in (early, late))
+    early, late = (all_but_last_sum(part, True) for part in (early, late))
     weights, own_gram = steps_weights(early, late, keep)
     other_gram = flip(own_gram, "tm", 1)
     piece = rows // PIECES
@@ -497,7 +508,7 @@
     cross = pair_gram(owns[0], others[0])
     for own, other in zip(owns[1:], others[1:]):
         cross = pair_gram(own, other, cross)
-    final = merge_weights(*all_but_last_sum(cross, "rows", False), own_gram, other_gram)
+    final = merge_weights(*all_but_last_sum(cross, False), own_gram, other_gram)
     return output(final, owns, others).T
 
 

time: 82.9 us -> 79.1 us (0.954)
  starting transfers between devices: 23.8 us -> 20.2 us
    ppermute x14 -> x5, starting transfers between devices: 23.8 us -> 1.9 us  [flip(): return lax.ppermute(block, axis, [(i, i ^ mask) for i in range(count)])]
    ppermute x0 -> x9, starting transfers between devices: none -> 18.3 us  [hop(): return lax.ppermute(block, ('tm', 'rows'), route)]
    ppermute x14 -> x5, waiting for transfers between devices: 12.5 us -> 0.82 us  [flip(): return lax.ppermute(block, axis, [(i, i ^ mask) for i in range(count)])]
    ppermute x0 -> x9, waiting for transfers between devices: none -> 11.4 us  [hop(): return lax.ppermute(block, ('tm', 'rows'), route)]
  transfers between devices with their start and end apart: 14 -> 14, of which waited for: 7 -> 8; matrix products, arithmetic and copies ran while one was open for 0% -> 0% of each run, Pallas kernels for 18% -> 19%
where the time goes in v5:
time: 79.1 us; the launch traced here: 79 us
  Pallas kernels  46.2 us (58%)
  starting transfers between devices  20.2 us (26%)
  waiting for transfers between devices  12.2 us (15%)
    pallas_call x2, Pallas kernels, call(): pl.pallas_call(kernel, out_shape=tuple((jax.ShapeDtypeStruct(shape, F32)...  19.9 us
    ppermute x9, starting transfers between devices, hop(): return lax.ppermute(block, ('tm', 'rows'), route)  18.3 us
    pallas_call x1, Pallas kernels, local_gram(): pl.pallas_call(functools.partial(gram_kernel, cuts), out_shape=(pltpu.VME...  12.5 us
    ppermute x9, waiting for transfers between devices, hop(): return lax.ppermute(block, ('tm', 'rows'), route)  11.4 us
    pallas_call x4, Pallas kernels, project(): pl.pallas_call(functools.partial(modes_kernel, first), out_shape=pltpu.VM...  5.38 us
    pallas_call x1, Pallas kernels, merge_weights(): pl.pallas_call(merge_kernel, out_shape=jax.ShapeDtypeStruct((keep // 2, 2...  4.27 us
    pallas_call x1, Pallas kernels, output(): pl.pallas_call(functools.partial(output_kernel, len(owns)), out_shape=jax...  2.15 us
    pallas_call x4, Pallas kernels, pair_gram(): pl.pallas_call(pair_kernel, out_shape=jax.ShapeDtypeStruct((keep // 2, 2...  1.93 us
  transfers between devices with their start and end apart: 14, of which 8 were waited for; matrix products, arithmetic and copies ran while one was open for 0% of the time, Pallas kernels for 19%

profile of v5, /device:TPU:0, one launch (start us, length us, event | category | flops | bytes accessed | tf_op | source)
XLA Modules:
  0.0 79.0 jit_solution(15013751715494618081)
XLA Ops:
  0.0 12.5 %gram.1 = (f32[64,384]{1,0:T(8,128)S(1)}, f32[64,512]{1,0:T(8,128)S(1)}, bf16[64,32768]{1,0:T(8,128)(2,1)S(1)}, bf16[32768,256]{1,0:T(8,128)(2,1)S(1)}) custom-call(bf16[64,32768]{1,0:T(8,128)(2,1)} %bitcast.6, bf16[32768,256]{1,0:T(8,128)(2,1)} %bitcast.5), custom_call_target="tpu_custom_call" | custom-call | tf_op jit(solution)/shard_map/gram/pallas_call | solution.py:322
  12.6 3.1 %collective-permute-start = (f32[64,384]{1,0:T(8,128)S(1)}, f32[64,384]{1,0:T(8,128)S(1)}, u32[]{:S(2)}, u32[]{:S(2)}) collective-permute-start(f32[64,384]{1,0:T(8,128)S(1)} %get-tuple-element.11), channel_id=1, source_target_pairs={{0,1},{1,0},{2,3},{3,2},{4,5},{5,4},{6,7},{7,6},{8,10},{9,11},{10,... | collective-permute-start | bytes 294920 | tf_op jit(solution)/shard_map/ppermute | solution.py:468
  15.7 2.5 %collective-permute-done = f32[64,384]{1,0:T(8,128)S(1)} collective-permute-done((f32[64,384]{1,0:T(8,128)S(1)}, f32[64,384]{1,0:T(8,128)S(1)}, u32[]{:S(2)}, u32[]{:S(2)}) %collective-permute-start) | collective-permute-done | bytes 98336 | tf_op jit(solution)/shard_map/ppermute | solution.py:468
  18.2 2.1 %collective-permute-start.1 = (f32[64,384]{1,0:T(8,128)S(1)}, f32[64,384]{1,0:T(8,128)S(1)}, u32[]{:S(2)}, u32[]{:S(2)}) collective-permute-start(f32[64,384]{1,0:T(8,128)S(1)} %add.18), channel_id=1, source_target_pairs={{0,2},{1,3},{2,0},{3,1},{4,6},{5,7},{6,4},{7,5},{8,14},{9,15},{10,... | collective-permute-start | bytes 294920 | tf_op jit(solution)/shard_map/ppermute | solution.py:468
  20.4 0.2 collective-permute-done.3
  20.6 1.6 %collective-permute-start.4 = (f32[64,512]{1,0:T(8,128)S(1)}, f32[64,512]{1,0:T(8,128)S(1)}, u32[]{:S(2)}, u32[]{:S(2)}) collective-permute-start(f32[64,512]{1,0:T(8,128)S(1)} %add.20), channel_id=1, source_target_pairs={{0,2},{1,3},{2,0},{3,1},{4,6},{5,7},{6,4},{7,5},{8,14},{9,15},{10,... | collective-permute-start | bytes 393224 | tf_op jit(solution)/shard_map/ppermute | solution.py:468
  22.3 1.8 %collective-permute-done.1 = f32[64,384]{1,0:T(8,128)S(1)} collective-permute-done((f32[64,384]{1,0:T(8,128)S(1)}, f32[64,384]{1,0:T(8,128)S(1)}, u32[]{:S(2)}, u32[]{:S(2)}) %collective-permute-start.1) | collective-permute-done | bytes 98336 | tf_op jit(solution)/shard_map/ppermute | solution.py:468
  24.0 4.1 %collective-permute-start.2 = (f32[64,384]{1,0:T(8,128)S(1)}, f32[64,384]{1,0:T(8,128)S(1)}, u32[]{:S(2)}, u32[]{:S(2)}) collective-permute-start(f32[64,384]{1,0:T(8,128)S(1)} %add.19.left_ref), channel_id=1, source_target_pairs={{0,6},{1,7},{2,4},{3,5},{4,2},{5,3},{6,0},{7,1},{8,9},{9,8},{10,11... | collective-permute-start | bytes 294920 | tf_op jit(solution)/shard_map/ppermute | solution.py:468
  28.2 2.4 %collective-permute-start.5 = (f32[64,512]{1,0:T(8,128)S(1)}, f32[64,512]{1,0:T(8,128)S(1)}, u32[]{:S(2)}, u32[]{:S(2)}) collective-permute-start(f32[64,512]{1,0:T(8,128)S(1)} %add.21.late_left), channel_id=1, source_target_pairs={{0,6},{1,7},{2,4},{3,5},{4,2},{5,3},{6,0},{7,1},{8,9},{9,8},{10,11... | collective-permute-start | bytes 393224 | tf_op jit(solution)/shard_map/ppermute | solution.py:468
  30.6 0.3 collective-permute-done.2.right_ref
  30.8 9.3 %steps.2.before_ref = f32[64,256]{1,0:T(8,128)S(1)} custom-call(f32[64,384]{1,0:T(8,128)S(1)} %add.19.left_ref, f32[64,384]{1,0:T(8,128)S(1)} %collective-permute-done.2.right_ref), custom_call_target="tpu_custom_call" | custom-call | flops 10000000000 | bytes 1048576 | tf_op jit(solution)/shard_map/steps/pallas_call | solution.py:249
  40.2 10.6 %steps.3 = (f32[64,384]{1,0:T(8,128)S(1)}, f32[64,64]{1,0:T(8,128)S(1)}) custom-call(f32[64,384]{1,0:T(8,128)S(1)} %add.19.left_ref, f32[64,384]{1,0:T(8,128)S(1)} %collective-permute-done.2.right_ref, f32[64,512]{1,0:T(8,128)S(1)} %add.21.late_left, f32[64,512]{1,0:T(8,128)S(1)} %collective-permute-done.5.late_right, f32[64,256]{1,0:T(8,128)S(1)} %steps.2.before_ref), custom_call_target="tpu_custom_call" | custom-call | flops 10000000000 | bytes 1048576 | tf_op jit(solution)/shard_map/steps/pallas_call | solution.py:249
  50.7 1.3 %project.7.own_ref.refs_0_ = bf16[64,8192]{1,0:T(8,128)(2,1)S(1)} custom-call(f32[64,384]{1,0:T(8,128)S(1)} %get-tuple-element.13.weights_ref, bf16[64,32768]{1,0:T(8,128)(2,1)S(1)} %get-tuple-element.14.prior_ref, bf16[32768,256]{1,0:T(8,128)(2,1)S(1)} %get-tuple-element.15.frames_ref), custom_call_target="tpu_custom_call" | custom-call | tf_op jit(solution)/shard_map/project/pallas_call | solution.py:362
  52.2 1.3 %project.6.own_ref.refs_1_ = bf16[64,8192]{1,0:T(8,128)(2,1)S(1)} custom-call(f32[64,384]{1,0:T(8,128)S(1)} %get-tuple-element.13.weights_ref, bf16[64,32768]{1,0:T(8,128)(2,1)S(1)} %get-tuple-element.14.prior_ref, bf16[32768,256]{1,0:T(8,128)(2,1)S(1)} %get-tuple-element.15.frames_ref), custom_call_target="tpu_custom_call" | custom-call | tf_op jit(solution)/shard_map/project/pallas_call | solution.py:362
  53.5 0.6 collective-permute-start.8
  54.1 1.3 %project.5.own_ref.refs_2_ = bf16[64,8192]{1,0:T(8,128)(2,1)S(1)} custom-call(f32[64,384]{1,0:T(8,128)S(1)} %get-tuple-element.13.weights_ref, bf16[64,32768]{1,0:T(8,128)(2,1)S(1)} %get-tuple-element.14.prior_ref, bf16[32768,256]{1,0:T(8,128)(2,1)S(1)} %get-tuple-element.15.frames_ref), custom_call_target="tpu_custom_call" | custom-call | tf_op jit(solution)/shard_map/project/pallas_call | solution.py:362
  55.5 1.3 %project.4.own_ref.refs_3_ = bf16[64,8192]{1,0:T(8,128)(2,1)S(1)} custom-call(f32[64,384]{1,0:T(8,128)S(1)} %get-tuple-element.13.weights_ref, bf16[64,32768]{1,0:T(8,128)(2,1)S(1)} %get-tuple-element.14.prior_ref, bf16[32768,256]{1,0:T(8,128)(2,1)S(1)} %get-tuple-element.15.frames_ref), custom_call_target="tpu_custom_call" | custom-call | tf_op jit(solution)/shard_map/project/pallas_call | solution.py:362
  56.9 0.6 collective-permute-start.6
  57.4 0.5 pair.4.rest_0_
  57.9 0.5 pair.5.rest_0_
  58.4 0.5 pair.6.rest_0_
  58.9 0.8 %collective-permute-done.6.other_ref.refs_7_ = bf16[64,8192]{1,0:T(8,128)(2,1)S(1)} collective-permute-done((bf16[64,8192]{1,0:T(8,128)(2,1)S(1)}, bf16[64,8192]{1,0:T(8,128)(2,1)S(1)}, u32[]{:S(2)}, u32[]{:S(2)}) %collective-permute-start.6) | collective-permute-done | bytes 1048608 | tf_op jit(solution)/shard_map/ppermute | solution.py:460
  59.7 0.5 pair.7
  60.2 1.5 %collective-permute-start.10 = (f32[32,128]{1,0:T(8,128)S(1)}, f32[32,128]{1,0:T(8,128)S(1)}, u32[]{:S(2)}, u32[]{:S(2)}) collective-permute-start(f32[32,128]{1,0:T(8,128)S(1)} %pair.7), channel_id=1, source_target_pairs={{0,1},{1,0},{2,3},{3,2},{4,5},{5,4},{6,7},{7,6},{8,10},{9,11},{10,... | collective-permute-start | bytes 49160 | tf_op jit(solution)/shard_map/ppermute | solution.py:468
  61.7 2.2 %collective-permute-done.10 = f32[32,128]{1,0:T(8,128)S(1)} collective-permute-done((f32[32,128]{1,0:T(8,128)S(1)}, f32[32,128]{1,0:T(8,128)S(1)}, u32[]{:S(2)}, u32[]{:S(2)}) %collective-permute-start.10) | collective-permute-done | bytes 16416 | tf_op jit(solution)/shard_map/ppermute | solution.py:468
  64.0 1.0 %collective-permute-start.11 = (f32[32,128]{1,0:T(8,128)S(1)}, f32[32,128]{1,0:T(8,128)S(1)}, u32[]{:S(2)}, u32[]{:S(2)}) collective-permute-start(f32[32,128]{1,0:T(8,128)S(1)} %add.22), channel_id=1, source_target_pairs={{0,2},{1,3},{2,0},{3,1},{4,6},{5,7},{6,4},{7,5},{8,12},{9,13},{10,... | collective-permute-start | bytes 49160 | tf_op jit(solution)/shard_map/ppermute | solution.py:468
  64.9 0.6 collective-permute-start.13
  65.5 2.2 %collective-permute-done.11 = f32[32,128]{1,0:T(8,128)S(1)} collective-permute-done((f32[32,128]{1,0:T(8,128)S(1)}, f32[32,128]{1,0:T(8,128)S(1)}, u32[]{:S(2)}, u32[]{:S(2)}) %collective-permute-start.11) | collective-permute-done | bytes 16416 | tf_op jit(solution)/shard_map/ppermute | solution.py:468
  67.7 2.4 %collective-permute-start.12 = (f32[32,128]{1,0:T(8,128)S(1)}, f32[32,128]{1,0:T(8,128)S(1)}, u32[]{:S(2)}, u32[]{:S(2)}) collective-permute-start(f32[32,128]{1,0:T(8,128)S(1)} %add.23.left_ref), channel_id=1, source_target_pairs={{0,4},{1,5},{2,6},{3,7},{4,0},{5,1},{6,2},{7,3},{8,9},{9,8},{10,11... | collective-permute-start | bytes 49160 | tf_op jit(solution)/shard_map/ppermute | solution.py:468
  70.1 2.3 %collective-permute-done.12.right_ref = f32[32,128]{1,0:T(8,128)S(1)} collective-permute-done((f32[32,128]{1,0:T(8,128)S(1)}, f32[32,128]{1,0:T(8,128)S(1)}, u32[]{:S(2)}, u32[]{:S(2)}) %collective-permute-start.12) | collective-permute-done | bytes 16416 | tf_op jit(solution)/shard_map/ppermute | solution.py:468
  72.3 4.3 %merge.1.weights_ref = f32[32,128]{1,0:T(8,128)S(1)} custom-call(f32[32,128]{1,0:T(8,128)S(1)} %add.23.left_ref, f32[32,128]{1,0:T(8,128)S(1)} %collective-permute-done.12.right_ref, f32[64,64]{1,0:T(8,128)S(1)} %get-tuple-element.16.own_ref, f32[64,64]{1,0:T(8,128)S(1)} %collective-permute-done.13.other_ref), custom_call_target="tpu_custom_call" | custom-call | tf_op jit(solution)/shard_map/merge/pallas_call | solution.py:414
  76.6 2.2 %output.1 = bf16[32,32768]{1,0:T(8,128)(2,1)} custom-call(f32[32,128]{1,0:T(8,128)S(1)} %merge.1.weights_ref, bf16[64,8192]{1,0:T(8,128)(2,1)S(1)} %project.7.own_ref.refs_0_, bf16[64,8192]{1,0:T(8,128)(2,1)S(1)} %project.6.own_ref.refs_1_, bf16[64,8192]{1,0:T(8,128)(2,1)S(1)} %project.5.own_ref.refs_2_, bf16[64,8192]{1,0:T(8,128)(2,1)S(1)} %project.4.own_ref.refs_3_, ...), custom_call_target="tpu_custom_call" | custom-call | tf_op jit(solution)/shard_map/output/pallas_call | solution.py:447
  (15 shorter events, 0.3 us)
Async XLA Ops:
  12.6 5.7 %collective-permute-start = (f32[64,384]{1,0:T(8,128)S(1)}, f32[64,384]{1,0:T(8,128)S(1)}, u32[]{:S(2)}, u32[]{:S(2)}) collective-permute-start(f32[64,384]{1,0:T(8,128)S(1)} %get-tuple-element.11), channel_id=1, source_target_pairs={{0,1},{1,0},{2,3},{3,2},{4,5},{5,4},{6,7},{7,6},{8,10},{9,11},{10,... | collective-permute-start | bytes 294920 | tf_op jit(solution)/shard_map/ppermute | solution.py:468
  15.6 5.0 %collective-permute-start.3 = (f32[64,512]{1,0:T(8,128)S(1)}, f32[64,512]{1,0:T(8,128)S(1)}, u32[]{:S(2)}, u32[]{:S(2)}) collective-permute-start(f32[64,512]{1,0:T(8,128)S(1)} %get-tuple-element.12), channel_id=1, source_target_pairs={{0,1},{1,0},{2,3},{3,2},{4,5},{5,4},{6,7},{7,6},{8,10},{9,11},{10,... | collective-permute-start | bytes 393224 | tf_op jit(solution)/shard_map/ppermute | solution.py:468
  18.2 5.8 %collective-permute-start.1 = (f32[64,384]{1,0:T(8,128)S(1)}, f32[64,384]{1,0:T(8,128)S(1)}, u32[]{:S(2)}, u32[]{:S(2)}) collective-permute-start(f32[64,384]{1,0:T(8,128)S(1)} %add.18), channel_id=1, source_target_pairs={{0,2},{1,3},{2,0},{3,1},{4,6},{5,7},{6,4},{7,5},{8,14},{9,15},{10,... | collective-permute-start | bytes 294920 | tf_op jit(solution)/shard_map/ppermute | solution.py:468
  20.6 7.5 %collective-permute-start.4 = (f32[64,512]{1,0:T(8,128)S(1)}, f32[64,512]{1,0:T(8,128)S(1)}, u32[]{:S(2)}, u32[]{:S(2)}) collective-permute-start(f32[64,512]{1,0:T(8,128)S(1)} %add.20), channel_id=1, source_target_pairs={{0,2},{1,3},{2,0},{3,1},{4,6},{5,7},{6,4},{7,5},{8,14},{9,15},{10,... | collective-permute-start | bytes 393224 | tf_op jit(solution)/shard_map/ppermute | solution.py:468
  24.0 6.8 %collective-permute-start.2 = (f32[64,384]{1,0:T(8,128)S(1)}, f32[64,384]{1,0:T(8,128)S(1)}, u32[]{:S(2)}, u32[]{:S(2)}) collective-permute-start(f32[64,384]{1,0:T(8,128)S(1)} %add.19.left_ref), channel_id=1, source_target_pairs={{0,6},{1,7},{2,4},{3,5},{4,2},{5,3},{6,0},{7,1},{8,9},{9,8},{10,11... | collective-permute-start | bytes 294920 | tf_op jit(solution)/shard_map/ppermute | solution.py:468
  28.2 12.0 %collective-permute-start.5 = (f32[64,512]{1,0:T(8,128)S(1)}, f32[64,512]{1,0:T(8,128)S(1)}, u32[]{:S(2)}, u32[]{:S(2)}) collective-permute-start(f32[64,512]{1,0:T(8,128)S(1)} %add.21.late_left), channel_id=1, source_target_pairs={{0,6},{1,7},{2,4},{3,5},{4,2},{5,3},{6,0},{7,1},{8,9},{9,8},{10,11... | collective-permute-start | bytes 393224 | tf_op jit(solution)/shard_map/ppermute | solution.py:468
  52.1 5.3 %collective-permute-start.9 = (bf16[64,8192]{1,0:T(8,128)(2,1)S(1)}, bf16[64,8192]{1,0:T(8,128)(2,1)S(1)}, u32[]{:S(2)}, u32[]{:S(2)}) collective-permute-start(bf16[64,8192]{1,0:T(8,128)(2,1)S(1)} %project.7.own_ref.refs_0_), channel_id=1, source_target_pairs={{0,8},{8,0},{1,9},{9,1},{2,10},{10,2},{3,11},{11,3},{4,12},{12,4},... | collective-permute-start | bytes 3145736 | tf_op jit(solution)/shard_map/ppermute | solution.py:460
  53.5 4.4 %collective-permute-start.8 = (bf16[64,8192]{1,0:T(8,128)(2,1)S(1)}, bf16[64,8192]{1,0:T(8,128)(2,1)S(1)}, u32[]{:S(2)}, u32[]{:S(2)}) collective-permute-start(bf16[64,8192]{1,0:T(8,128)(2,1)S(1)} %project.6.own_ref.refs_1_), channel_id=1, source_target_pairs={{0,8},{8,0},{1,9},{9,1},{2,10},{10,2},{3,11},{11,3},{4,12},{12,4},... | collective-permute-start | bytes 3145736 | tf_op jit(solution)/shard_map/ppermute | solution.py:460
  55.4 3.0 %collective-permute-start.7 = (bf16[64,8192]{1,0:T(8,128)(2,1)S(1)}, bf16[64,8192]{1,0:T(8,128)(2,1)S(1)}, u32[]{:S(2)}, u32[]{:S(2)}) collective-permute-start(bf16[64,8192]{1,0:T(8,128)(2,1)S(1)} %project.5.own_ref.refs_2_), channel_id=1, source_target_pairs={{0,8},{8,0},{1,9},{9,1},{2,10},{10,2},{3,11},{11,3},{4,12},{12,4},... | collective-permute-start | bytes 3145736 | tf_op jit(solution)/shard_map/ppermute | solution.py:460
  56.9 2.8 %collective-permute-start.6 = (bf16[64,8192]{1,0:T(8,128)(2,1)S(1)}, bf16[64,8192]{1,0:T(8,128)(2,1)S(1)}, u32[]{:S(2)}, u32[]{:S(2)}) collective-permute-start(bf16[64,8192]{1,0:T(8,128)(2,1)S(1)} %project.4.own_ref.refs_3_), channel_id=1, source_target_pairs={{0,8},{8,0},{1,9},{9,1},{2,10},{10,2},{3,11},{11,3},{4,12},{12,4},... | collective-permute-start | bytes 3145736 | tf_op jit(solution)/shard_map/ppermute | solution.py:460
  60.2 3.8 %collective-permute-start.10 = (f32[32,128]{1,0:T(8,128)S(1)}, f32[32,128]{1,0:T(8,128)S(1)}, u32[]{:S(2)}, u32[]{:S(2)}) collective-permute-start(f32[32,128]{1,0:T(8,128)S(1)} %pair.7), channel_id=1, source_target_pairs={{0,1},{1,0},{2,3},{3,2},{4,5},{5,4},{6,7},{7,6},{8,10},{9,11},{10,... | collective-permute-start | bytes 49160 | tf_op jit(solution)/shard_map/ppermute | solution.py:468
  64.0 3.7 %collective-permute-start.11 = (f32[32,128]{1,0:T(8,128)S(1)}, f32[32,128]{1,0:T(8,128)S(1)}, u32[]{:S(2)}, u32[]{:S(2)}) collective-permute-start(f32[32,128]{1,0:T(8,128)S(1)} %add.22), channel_id=1, source_target_pairs={{0,2},{1,3},{2,0},{3,1},{4,6},{5,7},{6,4},{7,5},{8,12},{9,13},{10,... | collective-permute-start | bytes 49160 | tf_op jit(solution)/shard_map/ppermute | solution.py:468
  64.9 5.1 %collective-permute-start.13 = (f32[64,64]{1,0:T(8,128)S(1)}, f32[64,64]{1,0:T(8,128)S(1)}, u32[]{:S(2)}, u32[]{:S(2)}) collective-permute-start(f32[64,64]{1,0:T(8,128)S(1)} %get-tuple-element.16.own_ref), channel_id=1, source_target_pairs={{0,8},{8,0},{1,9},{9,1},{2,10},{10,2},{3,11},{11,3},{4,12},{12,4},... | collective-permute-start | bytes 49160 | tf_op jit(solution)/shard_map/ppermute | solution.py:460
  67.7 4.6 %collective-permute-start.12 = (f32[32,128]{1,0:T(8,128)S(1)}, f32[32,128]{1,0:T(8,128)S(1)}, u32[]{:S(2)}, u32[]{:S(2)}) collective-permute-start(f32[32,128]{1,0:T(8,128)S(1)} %add.23.left_ref), channel_id=1, source_target_pairs={{0,4},{1,5},{2,6},{3,7},{4,0},{5,1},{6,2},{7,3},{8,9},{9,8},{10,11... | collective-permute-start | bytes 49160 | tf_op jit(solution)/shard_map/ppermute | solution.py:468
